TPU v7x, 32 devices: a whole 2x2x4 slice. The times are simulated.
32 devices in a mesh: orb: 16 (over z, y, core), grid: 2 (over x).
Axes of the slice: x: 2, y: 2, z: 4, core: 2. Of those that a mesh axis runs over, the one named last changes fastest.
Arguments:
- orbitals: bfloat16 [32, 11520], P('orb', 'grid'), may hold values from -1.5 to 1.5
- occupation: bfloat16 [32], P('orb'), may hold values from 0.29882812 to 1
Outputs:
- potentials: float32 [32, 11520], P('orb', 'grid')
- projectors: float32 [32, 11520], P('orb', 'grid')
All inputs are finite; a program needn't handle non-finite values.
Results may differ from a plain program's by a relative error of at most 0.0025.
Values may be sent and summed in bfloat16 or wider, within the bound.
No kernel may reach another device: no remote copies, remote signals or barrier semaphores. Data moves between devices by JAX's collectives and lax.ppermute only.
A program may use at most 64 MiB of HBM per device.

v0:
```python
import math

import jax
import jax.numpy as jnp
from jax import lax
from jax.sharding import PartitionSpec as P

NX = 20
NY = 24
NZ = 24
NPTS = 11520


def hartley_table(length):
    index = jnp.arange(length, dtype=jnp.int32)
    product = index[:, None] * index[None, :] % length
    angle = 2.0 * math.pi / length * product.astype(jnp.float32)
    return (jnp.cos(angle) + jnp.sin(angle)).astype(jnp.bfloat16)


def signed_square(length):
    index = jnp.arange(length, dtype=jnp.int32)
    signed = jnp.where(index <= length // 2, index, index - length).astype(jnp.float32)
    return (2.0 * math.pi * signed / length) ** 2


def coulomb_kernel(size_x, size_y, size_z):
    total = (
        signed_square(size_x)[:, None, None]
        + signed_square(size_y)[None, :, None]
        + signed_square(size_z)[None, None, :]
    )
    safe = jnp.where(total > 0, total, 1.0)
    return jnp.where(total > 0, 1.0 / safe, 0.0) / (size_x * size_y * size_z)


def solve_pairs(density, table_x, table_y, table_z, kernel):
    section = jnp.einsum(
        "ax,pxyz->payz", table_x, density, preferred_element_type=jnp.float32
    ).astype(jnp.bfloat16)
    section = jnp.einsum(
        "by,pxyz->pxbz", table_y, section, preferred_element_type=jnp.float32
    ).astype(jnp.bfloat16)
    spectrum = jnp.einsum("cz,pxyz->pxyc", table_z, section, preferred_element_type=jnp.float32)
    section = (spectrum * kernel).astype(jnp.bfloat16)
    section = jnp.einsum(
        "cz,pxyz->pxyc", table_z, section, preferred_element_type=jnp.float32
    ).astype(jnp.bfloat16)
    section = jnp.einsum(
        "by,pxyz->pxbz", table_y, section, preferred_element_type=jnp.float32
    ).astype(jnp.bfloat16)
    return jnp.einsum("ax,pxyz->payz", table_x, section, preferred_element_type=jnp.float32)


def pair_folder(targets, running, pieces):
    table_x = hartley_table(NX)
    table_y = hartley_table(NY)
    table_z = hartley_table(NZ)
    kernel = coulomb_kernel(NX, NY, NZ)
    target_rows = targets.astype(jnp.float32)
    target_count = targets.shape[0]
    block, block_weight = pieces
    rows = block.shape[0]
    group = math.gcd(rows, 64)
    blocks = block.reshape(rows // group, group, NPTS)
    weights = block_weight.astype(jnp.float32).reshape(rows // group, group)

    def accumulate(totals, inputs):
        sources, source_weight = inputs
        source_rows = sources.astype(jnp.float32)
        density = (target_rows[:, None, :] * source_rows[None, :, :]).astype(jnp.bfloat16)
        density = density.reshape(target_count * group, NX, NY, NZ)
        potential = solve_pairs(density, table_x, table_y, table_z, kernel).reshape(
            target_count, group, NPTS
        )
        weighted = source_weight[None, :, None] * potential * source_rows[None, :, :]
        return (totals - jnp.sum(weighted, axis=1), None)

    result, unused = lax.scan(accumulate, running, (blocks, weights))
    return result


def on_device(orbitals, occupation):
    own_count = orbitals.shape[0]
    per_device = own_count // lax.axis_size("grid")
    empty = jnp.zeros((per_device, NPTS), jnp.float32)
    whole = lax.all_gather(orbitals, "grid", axis=1, tiled=True)
    targets = lax.dynamic_slice_in_dim(whole, lax.axis_index("grid") * per_device, per_device, 0)
    totals = pair_folder(
        targets,
        empty,
        (
            lax.all_gather(whole, "orb", axis=0, tiled=True),
            lax.all_gather(occupation, "orb", axis=0, tiled=True),
        ),
    )
    potentials = lax.all_to_all(totals, "grid", split_axis=1, concat_axis=0, tiled=True)
    source_points, potential_points = (
        lax.all_to_all(
            orbitals.astype(jnp.float32), "orb", split_axis=1, concat_axis=0, tiled=True
        ),
        lax.all_to_all(potentials, "orb", split_axis=1, concat_axis=0, tiled=True),
    )
    partial_gram = (
        lax.dot_general(
            source_points,
            potential_points,
            (((1,), (1,)), ((), ())),
            precision=lax.Precision.HIGHEST,
        )
        / NPTS
    )
    gram = lax.psum(partial_gram, ("orb", "grid"))
    factor = jnp.linalg.cholesky(-gram)
    identity = jnp.eye(gram.shape[0], dtype=jnp.float32)
    inverse = lax.linalg.triangular_solve(factor, identity, left_side=True, lower=True)
    projector_points = jnp.dot(inverse, potential_points, precision=lax.Precision.HIGHEST)
    projectors = lax.all_to_all(projector_points, "orb", split_axis=0, concat_axis=1, tiled=True)
    return (potentials, projectors)


def solution(mesh):
    placed = (P("orb", "grid"), P("orb"))
    return jax.shard_map(
        on_device,
        mesh=mesh,
        in_specs=placed,
        out_specs=(P("orb", "grid"), P("orb", "grid")),
        check_vma=False,
    )
```

profile of v0, /device:TPU:0, one launch (start us, length us, event | category | flops | bytes accessed | tf_op | source)
XLA Modules:
  0.0 226.1 jit_solution(919936937522886090)
XLA Ops:
  0.7 5.7 %all_gather.10 = bf16[2,11520]{1,0:T(2,128)(2,1)S(1)} all-gather(bf16[2,5760]{1,0:T(2,128)(2,1)} %param.2), channel_id=1, replica_groups=mesh['orb'=16,'grid'=2] {'grid'}, dimensions={1}, use_global_device_ids=true | all-gather | bytes 69120 | tf_op jit(solution)/shard_map/all_gather | solution.py:87
  6.3 24.3 %all-gather = bf16[16,2,11520]{2,1,0:T(2,128)(2,1)S(1)} all-gather(bf16[1,2,11520]{2,1,0:T(2,128)(2,1)S(1)} %bitcast.58), channel_id=1, replica_groups=mesh['orb'=16,'grid'=2] {'orb'}, dimensions={0}, use_global_device_ids=true | all-gather | bytes 783360 | tf_op jit(solution)/shard_map/all_gather | solution.py:93
  30.7 6.4 %reshape.167 = f32[32,20,24,24]{3,2,1,0:T(8,128)} reshape(bf16[16,2,11520]{2,1,0:T(2,128)(2,1)S(1)} %all-gather) | data formatting | bytes 2211840 | tf_op jit(solution)/shard_map/while/body/eval_jaxpr/convert_element_type | solution.py:70
  37.1 1.3 reshape.174
  38.4 0.1 convert_reduce_fusion
  38.6 0.2 reshape.166
  38.8 3.9 %multiply_convert_fusion.1 = bf16[32,20,24,24]{3,2,1,0:T(8,128)(2,1)S(1)} fusion(f32[32,20,24,24]{3,2,1,0:T(8,128)} %reshape.167, f32[20,24,24]{2,1,0:T(8,128)S(1)} %reshape.166), kind=kLoop, calls=%fused_computation.1 | loop fusion | flops 737280 | bytes 2257920 | tf_op jit(solution)/shard_map/while/body/eval_jaxpr/convert_element_type | solution.py:71
  42.6 4.9 %convert_bitcast_fusion = bf16[32,20,24,24]{1,3,2,0:T(8,128)(2,1)} fusion(bf16[32,20,24,24]{3,2,1,0:T(8,128)(2,1)S(1)} %multiply_convert_fusion.1), kind=kOutput, calls=%fused_computation.4 | convolution fusion | flops 15118640 | bytes 1474560 | tf_op jit(solution)/shard_map/while/body/eval_jaxpr/ax,pxyz->payz/dot_general | solution.py:38
  47.5 8.5 %copy.24 = bf16[32,20,24,24]{2,3,1,0:T(8,128)(2,1)} copy(bf16[32,20,24,24]{1,3,2,0:T(8,128)(2,1)} %convert_bitcast_fusion) | data formatting | bytes 1474560 | tf_op jit(solution)/shard_map/while/body/eval_jaxpr/convert_element_type | solution.py:40
  56.0 5.2 %fusion.44 = bf16[32,20,24,24]{3,2,1,0:T(8,128)(2,1)} fusion(bf16[32,20,24,24]{2,3,1,0:T(8,128)(2,1)} %copy.24), kind=kOutput, calls=%fused_computation.53 | convolution fusion | flops 17701056 | bytes 1474560 | tf_op jit(solution)/shard_map/while/body/eval_jaxpr/by,pxyz->pxbz/dot_general | solution.py:41
  61.2 0.1 broadcast_add_fusion
  61.3 0.1 fusion.19
  61.5 7.4 %fusion.2 = bf16[32,20,24,24]{3,2,1,0:T(8,128)(2,1)} fusion(f32[20,24,24]{2,1,0:T(8,128)S(1)} %fusion.19, bf16[32,20,24,24]{3,2,1,0:T(8,128)(2,1)} %fusion.44), kind=kOutput, calls=%fused_computation.5 | convolution fusion | flops 36139392 | bytes 1520640 | tf_op jit(solution)/shard_map/while/body/eval_jaxpr/cz,pxyz->pxyc/dot_general | solution.py:46
  68.9 5.4 %convert_bitcast_fusion.1 = bf16[32,20,24,24]{2,3,1,0:T(8,128)(2,1)} fusion(bf16[32,20,24,24]{3,2,1,0:T(8,128)(2,1)} %fusion.2), kind=kOutput, calls=%fused_computation.8 | convolution fusion | flops 18069696 | bytes 1474560 | tf_op jit(solution)/shard_map/while/body/eval_jaxpr/by,pxyz->pxbz/dot_general | solution.py:49
  74.3 10.1 %copy.27 = bf16[32,20,24,24]{0,1,3,2:T(8,128)(2,1)S(1)} copy(bf16[32,20,24,24]{2,3,1,0:T(8,128)(2,1)} %convert_bitcast_fusion.1) | data formatting | bytes 1474560 | tf_op jit(solution)/shard_map/while/body/eval_jaxpr/convert_element_type | solution.py:51
  84.4 4.0 %convolution_bitcast_fusion = f32[32,20,24,24]{0,1,3,2:T(8,128)} fusion(bf16[32,20,24,24]{0,1,3,2:T(8,128)(2,1)S(1)} %copy.27), kind=kOutput, calls=%fused_computation.13 | convolution fusion | flops 14750000 | bytes 2211840 | tf_op jit(solution)/shard_map/while/body/eval_jaxpr/ax,pxyz->payz/dot_general | solution.py:52
  88.4 0.0 copy-start.3
  88.4 0.0 copy-start.2
  88.4 12.1 %copy.28 = f32[32,20,24,24]{3,2,1,0:T(8,128)} copy(f32[32,20,24,24]{0,1,3,2:T(8,128)} %convolution_bitcast_fusion) | data formatting | bytes 2949120 | tf_op jit(solution)/shard_map/while/body/eval_jaxpr/ax,pxyz->payz/transpose | solution.py:52
  100.5 0.0 copy-done.3
  100.5 0.6 dynamic-slice
  101.8 0.0 copy-done.2
  101.8 0.2 dynamic-update-slice.3
  102.0 0.0 copy-start
  102.0 0.0 copy-start.1
  102.0 6.8 %reshape.165 = f32[32,11520]{1,0:T(8,128)S(1)} reshape(f32[32,20,24,24]{3,2,1,0:T(8,128)} %copy.28) | data formatting | bytes 2949120 | tf_op jit(solution)/shard_map/while/body/eval_jaxpr/reshape | solution.py:73
  108.9 29.9 %all-reduce = bf16[32]{0:T(256)(128)(2,1)S(1)} all-reduce(bf16[32]{0:T(256)(128)(2,1)S(1)} %dynamic-update-slice.3), channel_id=1, replica_groups=mesh['orb'=16,'grid'=2] {'orb'}, use_global_device_ids=true, to_apply=%add | all-reduce | flops 32 | bytes 128
  138.8 0.0 copy-done
  138.8 0.3 multiply_reduce_fusion
  139.1 0.7 sub.25
  139.7 3.3 %all-to-all-start = ((f32[1,2,5760]{2,0,1:T(1,128)}), f32[1,2,5760]{2,0,1:T(1,128)S(1)}, u32[]{:S(2)}, u32[]{:S(2)}) async-start(f32[1,2,5760]{2,0,1:T(1,128)} %sub.25), calls=%async_computation | async-start | bytes 92160 | tf_op jit(solution)/shard_map/all_to_all | solution.py:97
  143.0 0.0 copy-done.1
  143.0 0.1 reshape.168
  143.2 0.6 copy.30
  143.8 3.2 %all-to-all-done = f32[1,2,5760]{2,0,1:T(1,128)S(1)} async-done(((f32[1,2,5760]{2,0,1:T(1,128)}), f32[1,2,5760]{2,0,1:T(1,128)S(1)}, u32[]{:S(2)}, u32[]{:S(2)}) %all-to-all-start) | async-done | bytes 46112 | tf_op jit(solution)/shard_map/all_to_all | solution.py:97
  147.0 3.5 %all-to-all-start.2 = ((f32[2,16,360]{2,0,1:T(2,128)}), f32[2,16,360]{2,0,1:T(2,128)S(1)}, u32[]{:S(2)}, u32[]{:S(2)}) async-start(f32[2,16,360]{2,0,1:T(2,128)} %copy.30), calls=%async_computation.2 | async-start | bytes 98304 | tf_op jit(solution)/shard_map/all_to_all | solution.py:99
  150.5 0.1 reduce.11
  150.7 0.1 all_to_all.54
  150.8 0.6 copy.29
  151.4 5.8 %all-to-all-done.2 = f32[2,16,360]{2,0,1:T(2,128)S(1)} async-done(((f32[2,16,360]{2,0,1:T(2,128)}), f32[2,16,360]{2,0,1:T(2,128)S(1)}, u32[]{:S(2)}, u32[]{:S(2)}) %all-to-all-start.2) | async-done | bytes 46112 | tf_op jit(solution)/shard_map/all_to_all | solution.py:99
  157.3 3.5 %all-to-all-start.1 = ((f32[2,16,360]{2,0,1:T(2,128)}), f32[2,16,360]{2,0,1:T(2,128)S(1)}, u32[]{:S(2)}, u32[]{:S(2)}) async-start(f32[2,16,360]{2,0,1:T(2,128)} %copy.29), calls=%async_computation.1 | async-start | bytes 98304 | tf_op jit(solution)/shard_map/all_to_all | solution.py:102
  160.8 6.7 %all-to-all-done.1 = f32[2,16,360]{2,0,1:T(2,128)S(1)} async-done(((f32[2,16,360]{2,0,1:T(2,128)}), f32[2,16,360]{2,0,1:T(2,128)S(1)}, u32[]{:S(2)}, u32[]{:S(2)}) %all-to-all-start.1) | async-done | bytes 46112 | tf_op jit(solution)/shard_map/all_to_all | solution.py:102
  167.6 0.2 fusion.17
  167.8 38.0 %psum.7 = f32[32,32]{0,1:T(8,128)S(1)} all-reduce(f32[32,32]{0,1:T(8,128)S(1)} %fusion.17), channel_id=1, replica_groups=mesh['orb'=16,'grid'=2] {'orb','grid'}, use_global_device_ids=true, to_apply=%region_1.2 | all-reduce | flops 1024 | bytes 8192 | tf_op jit(solution)/shard_map/psum | solution.py:113
  205.8 0.1 copy.31
  205.8 2.9 %cholesky.17 = f32[32,32]{1,0:T(8,128)S(1)} custom-call(f32[32,32]{1,0:T(8,128)S(1)} %fusion.22), custom_call_target="Cholesky" | custom-call | tf_op jit(solution)/shard_map/jit(cholesky)/cholesky | solution.py:114
  208.8 0.6 compare_reduce_fusion
  209.4 0.7 fusion.21
  210.1 2.4 %custom-call.6 = f32[1,32,32]{1,2,0:T(8,128)S(1)} custom-call(f32[1,32,32]{2,1,0:T(8,128)S(1)} %fusion.21), custom_call_target="InvertDiagBlocksLowerTriangular" | custom-call | tf_op jit(solution)/shard_map/triangular_solve | solution.py:116
  212.5 0.1 copy.32
  212.6 0.2 fusion.23
  212.8 0.2 fusion.88
  213.0 0.6 copy.34
  213.6 5.0 %all-to-all-start.3 = ((f32[16,2,360]{2,1,0:T(2,128)}), f32[16,2,360]{2,1,0:T(2,128)S(1)}, u32[]{:S(2)}, u32[]{:S(2)}) async-start(f32[16,2,360]{2,1,0:T(2,128)} %copy.34), calls=%async_computation.3 | async-start | bytes 98304 | tf_op jit(solution)/shard_map/all_to_all | solution.py:118
  218.6 0.6 copy.48
  219.3 6.1 %all-to-all-done.3 = f32[16,2,360]{2,1,0:T(2,128)S(1)} async-done(((f32[16,2,360]{2,1,0:T(2,128)}), f32[16,2,360]{2,1,0:T(2,128)S(1)}, u32[]{:S(2)}, u32[]{:S(2)}) %all-to-all-start.3) | async-done | bytes 46112 | tf_op jit(solution)/shard_map/all_to_all | solution.py:118
  225.4 0.8 all_to_all.65
  (12 shorter events, 0.2 us)
Async XLA Ops:
  88.4 12.1 %copy-start.3 = (u32[32]{0:T(128)S(1)}, u32[32]{0:T(128)}, u32[]{:S(2)}) copy-start(u32[32]{0:T(128)} %constant.125) | copy-start | bytes 388
  88.4 13.4 %copy-start.2 = (bf16[2]{0:T(256)(128)(2,1)S(1)}, bf16[2]{0:T(256)(128)(2,1)}, u32[]{:S(2)}) copy-start(bf16[2]{0:T(256)(128)(2,1)} %param.3) | copy-start | bytes 16
  102.0 36.7 %copy-start = (f32[32,11520]{1,0:T(8,128)S(1)}, f32[32,11520]{1,0:T(8,128)}, u32[]{:S(2)}) copy-start(f32[32,11520]{1,0:T(8,128)} %reshape.174) | copy-start | bytes 4423684
  102.0 41.0 %copy-start.1 = (bf16[2,5760]{1,0:T(2,128)(2,1)S(1)}, bf16[2,5760]{1,0:T(2,128)(2,1)}, u32[]{:S(2)}) copy-start(bf16[2,5760]{1,0:T(2,128)(2,1)} %param.2) | copy-start | bytes 69124
  139.7 7.3 %all-to-all-start = ((f32[1,2,5760]{2,0,1:T(1,128)}), f32[1,2,5760]{2,0,1:T(1,128)S(1)}, u32[]{:S(2)}, u32[]{:S(2)}) async-start(f32[1,2,5760]{2,0,1:T(1,128)} %sub.25), calls=%async_computation | async-start | bytes 92160 | tf_op jit(solution)/shard_map/all_to_all | solution.py:97
  147.0 10.2 %all-to-all-start.2 = ((f32[2,16,360]{2,0,1:T(2,128)}), f32[2,16,360]{2,0,1:T(2,128)S(1)}, u32[]{:S(2)}, u32[]{:S(2)}) async-start(f32[2,16,360]{2,0,1:T(2,128)} %copy.30), calls=%async_computation.2 | async-start | bytes 98304 | tf_op jit(solution)/shard_map/all_to_all | solution.py:99
  157.3 10.2 %all-to-all-start.1 = ((f32[2,16,360]{2,0,1:T(2,128)}), f32[2,16,360]{2,0,1:T(2,128)S(1)}, u32[]{:S(2)}, u32[]{:S(2)}) async-start(f32[2,16,360]{2,0,1:T(2,128)} %copy.29), calls=%async_computation.1 | async-start | bytes 98304 | tf_op jit(solution)/shard_map/all_to_all | solution.py:102
  213.6 11.8 %all-to-all-start.3 = ((f32[16,2,360]{2,1,0:T(2,128)}), f32[16,2,360]{2,1,0:T(2,128)S(1)}, u32[]{:S(2)}, u32[]{:S(2)}) async-start(f32[16,2,360]{2,1,0:T(2,128)} %copy.34), calls=%async_computation.3 | async-start | bytes 98304 | tf_op jit(solution)/shard_map/all_to_all | solution.py:118
where the time goes:
time: 227 us; the launch traced here: 226 us
  blocking collectives  97.9 us (43%)
  local copies, waits for them, and re-layouts  50.8 us (22%)
  matrix products  27.5 us (12%)
  waiting for transfers between devices  21.9 us (10%)
  starting transfers between devices  15.3 us (7%)
  other arithmetic  11.4 us (5%)
    psum x1, blocking collectives, on_device(): gram = lax.psum(partial_gram, ('orb', 'grid'))  38 us
    unnamed x1, blocking collectives  29.9 us
    all_gather x1, blocking collectives, on_device(): lax.all_gather(whole, 'orb', axis=0, tiled=True)  24.3 us
    transpose x1, local copies, waits for them, and re-layouts, solve_pairs(): jnp.einsum('ax,pxyz->payz', table_x, section, preferred_element_type=jnp....  12.1 us
    dot_general x2, matrix products, solve_pairs(): jnp.einsum('by,pxyz->pxbz', table_y, section, preferred_element_type=jnp....  10.6 us
    convert_element_type x1, local copies, waits for them, and re-layouts, solve_pairs(): section = jnp.einsum('by,pxyz->pxbz', table_y, section, preferred_element...  10.1 us
    convert_element_type x1, local copies, waits for them, and re-layouts, solve_pairs(): section = jnp.einsum('ax,pxyz->payz', table_x, density, preferred_element...  8.51 us
    convert_element_type x2, local copies, waits for them, and re-layouts, accumulate(): source_rows = sources.astype(jnp.float32)  7.76 us
  transfers between devices with their start and end apart: 4, of which 4 were waited for; matrix products, arithmetic and copies ran while one was open for 1% of the time, Pallas kernels for 0%

commit v1 on v0

v1 whole, which is shorter than its diff:
```python
import functools
import math

import jax
import jax.numpy as jnp
import numpy as np
from jax import lax
from jax.experimental import pallas as pl
from jax.experimental.pallas import tpu as pltpu
from jax.sharding import PartitionSpec as P

NX = 20
NY = 24
NZ = 24
NPTS = NX * NY * NZ
PLANE = NY * NZ
BAND = 128 // NZ
BANDS = -(-NY // BAND)
WIDE = BANDS * 128
F32 = jnp.float32
BF16 = jnp.bfloat16


def hartley_table(length):
    index = np.arange(length)
    angle = 2.0 * np.pi / length * (index[:, None] * index[None, :] % length)
    return (np.cos(angle) + np.sin(angle)).astype(BF16).astype(np.float32)


def signed_square(length):
    index = np.arange(length)
    signed = np.where(index <= length // 2, index, index - length)
    return (2.0 * np.pi * signed / length) ** 2


def coulomb_kernel():
    total = (
        signed_square(NX)[:, None, None]
        + signed_square(NY)[None, :, None]
        + signed_square(NZ)[None, None, :]
    )
    safe = np.where(total > 0, total, 1.0)
    return np.where(total > 0, 1.0 / safe, 0.0) / NPTS


def row_stride(own, planes):
    stride = planes + 1
    while own * stride % 8:
        stride += 1
    return stride


def tables(own, parts, cluster):
    planes = NX // parts
    stride = row_stride(own, planes)
    rows = own * stride
    table_x, table_y, table_z = hartley_table(NX), hartley_table(NY), hartley_table(NZ)
    mix_x = np.zeros((cluster, parts, own, stride, cluster, parts, own, stride), np.float32)
    cut = table_x.reshape(parts, planes, parts, planes)
    for owner in range(cluster):
        for orbital in range(own):
            mix_x[owner, :, orbital, :planes, owner, :, orbital, :planes] = cut
    mix_x = mix_x.reshape(cluster * parts * rows, cluster * parts * rows)
    lane = np.arange(NY)[:, None] // BAND * 128 + np.arange(NY)[:, None] % BAND * NZ + np.arange(NZ)
    mix_y = np.zeros((PLANE, WIDE), np.float32)
    natural = np.arange(PLANE).reshape(NY, NZ)
    for z in range(NZ):
        mix_y[np.ix_(natural[:, z], lane[:, z])] = table_y
    mix_z = np.zeros((256, 256), np.float32)
    for half in range(2):
        for band in range(BAND):
            at = half * 128 + band * NZ
            mix_z[at : at + NZ, at : at + NZ] = table_z
    scale = np.zeros((parts, own, stride, WIDE), np.float32)
    scale[:, :, :planes, lane.reshape(-1)] = coulomb_kernel().reshape(parts, 1, planes, PLANE)
    return (
        mix_x.astype(BF16),
        mix_y.astype(BF16),
        mix_z.astype(BF16),
        np.ascontiguousarray(mix_y.T).astype(BF16),
        scale.reshape(parts, rows, WIDE),
    )


def dot(left, right):
    return lax.dot_general(left, right, (((1,), (0,)), ((), ())), preferred_element_type=F32)


def bands(sections, mix_z):
    pieces = []
    for start in range(0, WIDE, 256):
        stop = min(start + 256, WIDE)
        width = stop - start
        pieces.append(dot(sections[:, start:stop], mix_z[:width, :width]))
    return jnp.concatenate(pieces, axis=1)


def halves(block, stride):
    return jnp.concatenate([block[..., stride:, :], block[..., :stride, :]], axis=-2)


def pair_body(
    place, blocks, mix_x, mix_y, mix_z, mix_back, scale, sent, totals,
    *, own, parts, stride, planes, cluster, chunk, copies,
):
    owners = blocks.shape[0] // parts
    rows = own * stride
    owner = place[0]
    part = place[1]
    row = lax.broadcasted_iota(jnp.int32, (1, rows, PLANE), 1)
    first = row < stride
    mine = blocks[pl.ds(owner * parts, parts)].astype(F32)
    target = jnp.where(first == (part == 0), mine, halves(mine, stride))
    totals[...] = jnp.zeros_like(totals)
    group = cluster * parts * rows
    x_table = mix_x[...]
    z_table = mix_z[...]

    def step(index, carry):
        source = blocks[pl.ds(index * chunk * parts, chunk * parts)].astype(F32)
        source = source.reshape(chunk, parts, rows, PLANE)
        density = (source * target[None]).astype(BF16).reshape(chunk * parts * rows, PLANE)
        section = jnp.concatenate(
            [
                dot(x_table, density[at : at + group]).astype(BF16)
                for at in range(0, chunk * parts * rows, group)
            ]
        )
        section = dot(section, mix_y[...]).astype(BF16)
        spectrum = bands(section, z_table).reshape(chunk, parts, rows, WIDE)
        section = (spectrum * scale[...][None]).astype(BF16).reshape(chunk * parts * rows, WIDE)
        section = bands(section, z_table).astype(BF16)
        section = dot(section, mix_back[...]).astype(BF16)
        potential = jnp.concatenate(
            [
                dot(x_table, section[at : at + group])
                for at in range(0, chunk * parts * rows, group)
            ]
        ).reshape(chunk, parts, rows, PLANE)
        weight = jnp.where(
            first[None],
            source[:, :, planes : planes + 1, :],
            source[:, :, stride + planes : stride + planes + 1, :],
        )
        totals[...] -= jnp.sum(weight * potential * source, axis=0)
        return carry

    steps = owners // chunk
    if steps == 1:
        step(0, 0)
    else:
        lax.fori_loop(0, steps, step, 0)
    partial = totals[...]
    folded = partial + halves(partial, stride)

    norb = owners * own
    lane = lax.broadcasted_iota(jnp.int32, (chunk, norb), 1)
    slot = lax.broadcasted_iota(jnp.int32, (chunk, norb), 0)

    def overlap(index, line):
        source = blocks[pl.ds(index * chunk * parts, chunk * parts)].astype(F32)
        source = source.reshape(chunk, parts, rows, PLANE)
        product = jnp.sum(source * folded[None], axis=1)
        for orbital in range(own):
            wanted = first if orbital == 0 else jnp.logical_not(first)
            picked = jnp.sum(jnp.where(wanted, product, 0.0), axis=1)
            value = jnp.sum(picked, axis=1, keepdims=True) / NPTS
            at = (index * chunk + slot) * own + orbital
            line = line + jnp.sum(jnp.where(lane == at, value, 0.0), axis=0, keepdims=True)
        return line

    line = jnp.zeros((1, norb), F32)
    line = overlap(0, line) if steps == 1 else lax.fori_loop(0, steps, overlap, line)
    line = jnp.concatenate([line, jnp.zeros((1, PLANE - norb), F32)], axis=1)
    sent_rows = sent.shape[2]
    place_row = lax.broadcasted_iota(jnp.int32, (1, sent_rows, PLANE), 1)
    mixed = jnp.where(place_row == planes, line[None], folded[:, :sent_rows])
    for at in range(copies):
        sent[at] = mixed


def solve_body(place, received, potentials, projectors, work, *, own, parts, planes):
    norb = received.shape[0]
    owner = place[0]
    gram = received[:, planes, :norb]
    matrix = -0.5 * (gram + gram.T)
    row = lax.broadcasted_iota(jnp.int32, (norb, norb), 0)
    column = lax.broadcasted_iota(jnp.int32, (norb, norb), 1)
    right = jnp.where(row == column, 1.0, 0.0).astype(F32)

    def eliminate(k, left, right, pivot_row, right_row, pivot_column):
        pivot = jnp.sum(jnp.where(column[:1] == k, pivot_row, 0.0), axis=1, keepdims=True)
        factor = jnp.where(row[:, :1] > k, pivot_column / pivot, 0.0)
        return left - factor * pivot_row, right - factor * right_row

    if norb <= 32:
        left = matrix
        for k in range(norb):
            factor = jnp.where(row[:, :1] > k, left[:, k : k + 1] / left[k : k + 1, k : k + 1], 0.0)
            left, right = left - factor * left[k : k + 1], right - factor * right[k : k + 1]
    else:
        work[0] = matrix
        work[1] = right

        def step(k, carry):
            left = work[0]
            right = work[1]
            pivot_row = work[0, pl.ds(k, 1), :]
            right_row = work[1, pl.ds(k, 1), :]
            pivot_column = jnp.sum(jnp.where(column == k, left, 0.0), axis=1, keepdims=True)
            work[0], work[1] = eliminate(k, left, right, pivot_row, right_row, pivot_column)
            return carry

        lax.fori_loop(0, norb, step, 0)
        left = work[0]
        right = work[1]
    diagonal = jnp.sum(jnp.where(row == column, left, 0.0), axis=1, keepdims=True)
    work[0] = right * lax.rsqrt(diagonal)
    for orbital in range(own):
        potentials[orbital] = received[owner * own + orbital, :planes, :]
        weights = work[0, pl.ds(owner * own + orbital, 1), :]
        total = jnp.zeros((planes, PLANE), F32)
        for at in range(norb):
            total = total + weights[:, at : at + 1] * received[at, :planes, :]
        projectors[orbital] = total


def on_device(orbitals, occupation):
    own = orbitals.shape[0]
    owners = lax.axis_size("orb")
    parts = lax.axis_size("grid")
    devices = owners * parts
    planes = NX // parts
    stride = row_stride(own, planes)
    rows = own * stride
    cluster = math.gcd(owners, max(1, 256 // (parts * rows)))
    chunk = math.gcd(owners, 16)
    place = jnp.stack([lax.axis_index("orb"), lax.axis_index("grid")]).astype(jnp.int32)
    block = jnp.concatenate(
        [
            orbitals.reshape(own, planes, PLANE),
            jnp.broadcast_to(occupation[:, None, None], (own, stride - planes, PLANE)),
        ],
        axis=1,
    ).reshape(1, rows, PLANE)
    blocks = spread(jnp.broadcast_to(block, (devices, rows, PLANE)))
    vmem = pl.BlockSpec(memory_space=pltpu.VMEM)
    smem = pl.BlockSpec(memory_space=pltpu.SMEM)
    sent_rows = 16
    sent = pl.pallas_call(
        functools.partial(
            pair_body, own=own, parts=parts, stride=stride, planes=planes,
            cluster=cluster, chunk=chunk, copies=owners,
        ),
        out_shape=jax.ShapeDtypeStruct((owners, parts, sent_rows, PLANE), F32),
        in_specs=[smem] + [vmem] * 6,
        out_specs=vmem,
        scratch_shapes=[pltpu.VMEM((parts, rows, PLANE), F32)],
        name="pairs",
    )(place, blocks, *(jnp.asarray(item) for item in tables(own, parts, cluster)))
    received = spread(sent.reshape(devices, sent_rows, PLANE))
    norb = owners * own
    shape = jax.ShapeDtypeStruct((own, planes, PLANE), F32)
    potentials, projectors = pl.pallas_call(
        functools.partial(solve_body, own=own, parts=parts, planes=planes),
        out_shape=(shape, shape),
        in_specs=[smem, vmem],
        out_specs=(vmem, vmem),
        scratch_shapes=[pltpu.VMEM((2, norb, norb), F32)],
        name="solve",
    )(place, received)
    size = planes * PLANE
    return (potentials.reshape(own, size), projectors.reshape(own, size))


def spread(blocks):
    return lax.all_to_all(blocks, ("orb", "grid"), split_axis=0, concat_axis=0, tiled=True)


def solution(mesh):
    placed = (P("orb", "grid"), P("orb"))
    return jax.shard_map(
        on_device,
        mesh=mesh,
        in_specs=placed,
        out_specs=(P("orb", "grid"), P("orb", "grid")),
        check_vma=False,
    )
```

time: 227 us -> 88.2 us (0.39)
  blocking collectives: 97.9 us -> 35.9 us
  local copies, waits for them, and re-layouts: 50.8 us -> 6.81 us
  matrix products: 27.5 us -> 0 us
  Pallas kernels: 0 us -> 11.6 us
  other arithmetic: 11.4 us -> 0.69 us
  starting transfers between devices: 15.3 us -> 7.33 us
    psum x1 -> x0, blocking collectives: 38 us -> none  [on_device(): gram = lax.psum(partial_gram, ('orb', 'grid'))]
    all_to_all x0 -> x1, blocking collectives: none -> 35.9 us  [spread(): lax.all_to_all(blocks, ('orb', 'grid'), split_axis=0, concat_axis=0, tile...]
    all_gather x2 -> x0, blocking collectives: 30 us -> none  [the longest x1 24.3 us: on_device(): lax.all_gather(whole, 'orb', axis=0, tiled=True)]
    unnamed x1 -> x0, blocking collectives: 29.9 us -> none
    dot_general x7 -> x0, matrix products: 27.3 us -> none  [the longest x2 10.6 us: solve_pairs(): jnp.einsum('by,pxyz->pxbz', table_y, section, preferred_element_type=jnp....]
    convert_element_type x4 -> x0, local copies, waits for them, and re-layouts: 26.4 us -> none  [the longest x1 10.1 us: solve_pairs(): section = jnp.einsum('by,pxyz->pxbz', table_y, section, preferred_element...]
    transpose x1 -> x0, local copies, waits for them, and re-layouts: 12.1 us -> none  [solve_pairs(): jnp.einsum('ax,pxyz->payz', table_x, section, preferred_element_type=jnp....]
    pallas_call x0 -> x2, Pallas kernels: none -> 11.6 us  [the longest x1 6.66 us: on_device(): pl.pallas_call(functools.partial(pair_body, own=own, parts=parts, stride=...]
  transfers between devices with their start and end apart: 4 -> 1, of which waited for: 4 -> 1; matrix products, arithmetic and copies ran while one was open for 1% -> 1% of each run, Pallas kernels for 0% -> 0%
where the time goes in v1:
time: 88.2 us; the launch traced here: 87.1 us
  blocking collectives  35.9 us (41%)
  waiting for transfers between devices  24.1 us (27%)
  Pallas kernels  11.6 us (13%)
  starting transfers between devices  7.33 us (8%)
  local copies, waits for them, and re-layouts  6.81 us (8%)
    all_to_all x1, blocking collectives, spread(): lax.all_to_all(blocks, ('orb', 'grid'), split_axis=0, concat_axis=0, tile...  35.9 us
    all_to_all x1, waiting for transfers between devices, spread(): lax.all_to_all(blocks, ('orb', 'grid'), split_axis=0, concat_axis=0, tile...  24.1 us
    all_to_all x1, starting transfers between devices, spread(): lax.all_to_all(blocks, ('orb', 'grid'), split_axis=0, concat_axis=0, tile...  7.33 us
    pallas_call x1, Pallas kernels, on_device(): pl.pallas_call(functools.partial(pair_body, own=own, parts=parts, stride=...  6.66 us
    pallas_call x1, Pallas kernels, on_device(): pl.pallas_call(functools.partial(solve_body, own=own, parts=parts, planes...  4.95 us
    reshape x2, local copies, waits for them, and re-layouts, on_device(): return (potentials.reshape(own, size), projectors.reshape(own, size))  3.21 us
  transfers between devices with their start and end apart: 1, of which 1 were waited for; matrix products, arithmetic and copies ran while one was open for 1% of the time, Pallas kernels for 0%

profile of v1, /device:TPU:0, one launch (start us, length us, event | category | flops | bytes accessed | tf_op | source)
XLA Modules:
  0.0 87.1 jit_solution(13270018362193026078)
XLA Ops:
  0.6 0.8 reshape.19
  1.5 0.7 broadcast_in_dim.6
  2.2 1.0 %broadcast_in_dim.15 = bf16[32,24,576]{2,1,0:T(8,128)(2,1)} broadcast(bf16[24,576]{1,0:T(8,128)(2,1)S(1)} %broadcast_in_dim.14), dimensions={1,2} | broadcast | bytes 912384 | tf_op jit(solution)/shard_map/broadcast_in_dim | solution.py:246
  3.3 7.3 %all-to-all-start = ((bf16[32,24,576]{2,1,0:T(8,128)(2,1)}), bf16[32,24,576]{2,1,0:T(8,128)(2,1)S(1)}, u32[]{:S(2)}, u32[]{:S(2)}) async-start(bf16[32,24,576]{2,1,0:T(8,128)(2,1)} %broadcast_in_dim.15), calls=%async_computation | async-start | bytes 1966080 | tf_op jit(solution)/shard_map/all_to_all | solution.py:277
  10.6 0.7 pad_add_fusion.place
  11.3 24.1 %all-to-all-done.blocks = bf16[32,24,576]{2,1,0:T(8,128)(2,1)S(1)} async-done(((bf16[32,24,576]{2,1,0:T(8,128)(2,1)}), bf16[32,24,576]{2,1,0:T(8,128)(2,1)S(1)}, u32[]{:S(2)}, u32[]{:S(2)}) %all-to-all-start) | async-done | bytes 884768 | tf_op jit(solution)/shard_map/all_to_all | solution.py:277
  35.4 0.0 copy-start
  35.4 1.0 %copy-done = bf16[32,24,576]{2,1,0:T(8,128)(2,1)} copy-done((bf16[32,24,576]{2,1,0:T(8,128)(2,1)}, bf16[32,24,576]{2,1,0:T(8,128)(2,1)S(1)}, u32[]{:S(2)}) %copy-start) | copy-done | bytes 884760
  36.4 6.7 %pairs.1 = f32[16,2,16,576]{3,2,1,0:T(8,128)} custom-call(s32[2]{0:T(128)} %pad_add_fusion.place, bf16[32,24,576]{2,1,0:T(8,128)(2,1)} %copy-done, bf16[48,48]{1,0:T(8,128)(2,1)} %constant.18.clone.mix_x, bf16[576,640]{1,0:T(8,128)(2,1)} %constant.19.clone.mix_y, bf16[256,256]{1,0:T(8,128)(2,1)} %constant.20.clone.mix_z, ...), custom_call_target="tpu_custom_call" | custom-call | tf_op jit(solution)/shard_map/pairs/pallas_call | solution.py:250
  43.1 35.9 %all_to_all.10.received = f32[32,16,576]{2,1,0:T(8,128)} all-to-all(f32[32,16,576]{2,1,0:T(8,128)} %bitcast.3), channel_id=1, replica_groups=mesh['orb'=16,'grid'=2] {'orb','grid'}, dimensions={0} | all-to-all | bytes 2359296 | tf_op jit(solution)/shard_map/all_to_all | solution.py:277
  79.0 4.9 %solve.1 = (f32[2,10,576]{2,1,0:T(8,128)}, f32[2,10,576]{2,1,0:T(8,128)}) custom-call(s32[2]{0:T(128)} %pad_add_fusion.place, f32[32,16,576]{2,1,0:T(8,128)} %all_to_all.10.received), custom_call_target="tpu_custom_call" | custom-call | tf_op jit(solution)/shard_map/solve/pallas_call | solution.py:264
  83.9 1.6 %reshape.21 = f32[2,5760]{1,0:T(2,128)} reshape(f32[2,10,576]{2,1,0:T(8,128)} %get-tuple-element.4) | data formatting | bytes 92160 | tf_op jit(solution)/shard_map/reshape | solution.py:273
  85.5 1.6 %reshape.22 = f32[2,5760]{1,0:T(2,128)} reshape(f32[2,10,576]{2,1,0:T(8,128)} %get-tuple-element.5) | data formatting | bytes 92160 | tf_op jit(solution)/shard_map/reshape | solution.py:273
  (2 shorter events, 0.0 us)
Async XLA Ops:
  3.3 32.1 %all-to-all-start = ((bf16[32,24,576]{2,1,0:T(8,128)(2,1)}), bf16[32,24,576]{2,1,0:T(8,128)(2,1)S(1)}, u32[]{:S(2)}, u32[]{:S(2)}) async-start(bf16[32,24,576]{2,1,0:T(8,128)(2,1)} %broadcast_in_dim.15), calls=%async_computation | async-start | bytes 1966080 | tf_op jit(solution)/shard_map/all_to_all | solution.py:277
  35.4 1.0 %copy-start = (bf16[32,24,576]{2,1,0:T(8,128)(2,1)}, bf16[32,24,576]{2,1,0:T(8,128)(2,1)S(1)}, u32[]{:S(2)}) copy-start(bf16[32,24,576]{2,1,0:T(8,128)(2,1)S(1)} %all-to-all-done.blocks) | copy-start | bytes 2654212

commit v2 on v1

v2 whole, which is shorter than its diff:
```python
import functools
import math

import jax
import jax.numpy as jnp
import numpy as np
from jax import lax
from jax.experimental import pallas as pl
from jax.experimental.pallas import tpu as pltpu
from jax.sharding import PartitionSpec as P

NX = 20
NY = 24
NZ = 24
NPTS = NX * NY * NZ
PLANE = NY * NZ
BAND = 128 // NZ
BANDS = -(-NY // BAND)
WIDE = BANDS * 128
F32 = jnp.float32
BF16 = jnp.bfloat16


def hartley_table(length):
    index = np.arange(length)
    angle = 2.0 * np.pi / length * (index[:, None] * index[None, :] % length)
    return (np.cos(angle) + np.sin(angle)).astype(BF16).astype(np.float32)


def signed_square(length):
    index = np.arange(length)
    signed = np.where(index <= length // 2, index, index - length)
    return (2.0 * np.pi * signed / length) ** 2


def coulomb_kernel():
    total = (
        signed_square(NX)[:, None, None]
        + signed_square(NY)[None, :, None]
        + signed_square(NZ)[None, None, :]
    )
    safe = np.where(total > 0, total, 1.0)
    return np.where(total > 0, 1.0 / safe, 0.0) / NPTS


def row_stride(own, planes):
    stride = planes + 1
    while own * stride % 8:
        stride += 1
    return stride


def tables(own, parts, cluster):
    planes = NX // parts
    stride = row_stride(own, planes)
    rows = own * stride
    table_x, table_y, table_z = hartley_table(NX), hartley_table(NY), hartley_table(NZ)
    mix_x = np.zeros((parts,) + (parts, cluster, own, stride) * 2, np.float32)
    cut = table_x.reshape(parts, planes, parts, planes)
    for part in range(parts):
        order = [part ^ other for other in range(parts)]
        for owner in range(cluster):
            for orbital in range(own):
                mix_x[part, :, owner, orbital, :planes, :, owner, orbital, :planes] = cut[
                    order
                ][:, :, order].transpose(0, 1, 2, 3)
    mix_x = mix_x.reshape(parts, cluster * parts * rows, cluster * parts * rows)
    lane = np.arange(NY)[:, None] // BAND * 128 + np.arange(NY)[:, None] % BAND * NZ + np.arange(NZ)
    mix_y = np.zeros((PLANE, WIDE), np.float32)
    natural = np.arange(PLANE).reshape(NY, NZ)
    for z in range(NZ):
        mix_y[np.ix_(natural[:, z], lane[:, z])] = table_y
    mix_z = np.zeros((256, 256), np.float32)
    for half in range(2):
        for band in range(BAND):
            at = half * 128 + band * NZ
            mix_z[at : at + NZ, at : at + NZ] = table_z
    scale = np.zeros((parts, own, stride, WIDE), np.float32)
    scale[:, :, :planes, lane.reshape(-1)] = coulomb_kernel().reshape(parts, 1, planes, PLANE)
    return (
        mix_x.astype(BF16),
        mix_y.astype(BF16),
        mix_z.astype(BF16),
        np.ascontiguousarray(mix_y.T).astype(BF16),
        scale.reshape(parts, rows, WIDE),
    )


def dot(left, right):
    return lax.dot_general(left, right, (((1,), (0,)), ((), ())), preferred_element_type=F32)


def bands(sections, mix_z):
    pieces = []
    for start in range(0, WIDE, 256):
        stop = min(start + 256, WIDE)
        width = stop - start
        pieces.append(dot(sections[:, start:stop], mix_z[:width, :width]))
    return jnp.concatenate(pieces, axis=1)


def halves(block, stride):
    return jnp.concatenate([block[..., stride:, :], block[..., :stride, :]], axis=-2)


class Route:
    def __init__(self, devices):
        top = devices.bit_length() - 1
        rest = list(range(top - 1, 1, -1))
        rounds = [rest[:2], rest[2:3] + [0]]
        rounds += [rest[at : at + 2] for at in range(3, len(rest), 2)] + [[1]]
        self.devices = devices
        self.rounds = rounds
        self.bits = [bit for members in rounds for bit in reversed(members)]
        self.owner_bits = [bit - 1 for bit in self.bits if bit]
        self.cluster = 1 << len(rounds[0])

    def masks(self, members):
        order = list(reversed(members))
        return [
            sum((at >> t & 1) << bit for t, bit in enumerate(order))
            for at in range(1 << len(order))
        ]

    def swap(self, array, mask):
        pairs = [(at, at ^ mask) for at in range(self.devices)]
        return lax.ppermute(array, ("orb", "grid"), pairs)


def spell(position, bits):
    return sum((position >> t & 1) << bit for t, bit in enumerate(bits))


def pack_body(orbitals, occupation, block, *, own, planes, stride):
    values = orbitals[...].astype(F32)
    weights = occupation[...].astype(F32)
    lines = []
    for orbital in range(own):
        for x in range(planes):
            lines.append(values[orbital : orbital + 1, x * PLANE : (x + 1) * PLANE])
        lines.append(
            jnp.broadcast_to(weights[orbital : orbital + 1], (stride - planes, PLANE))
        )
    block[0] = jnp.concatenate(lines, axis=0).astype(BF16)


def target_of(part, local, own, stride, cluster):
    mine = jnp.stack([local[0], local[cluster]]).astype(F32)
    first = lax.broadcasted_iota(jnp.int32, mine.shape, 1) < stride
    return jnp.where(first == (part == 0), mine, halves(mine, stride))


def sources_of(blocks, index, chunk, parts, cluster):
    source = blocks[pl.ds(index * chunk, chunk)].astype(F32)
    return source.reshape((chunk // (parts * cluster), parts, cluster) + blocks.shape[1:])


def add_pairs(
    part, target, blocks, mix_x, mix_y, mix_z, mix_back, scale, totals,
    *, parts, stride, planes, cluster, chunk,
):
    rows = blocks.shape[1]
    group = parts * cluster * rows
    first = lax.broadcasted_iota(jnp.int32, (1, 1, 1, rows, PLANE), 3) < stride
    x_table = mix_x[part]
    z_table = mix_z[...]
    factor = jnp.stack([scale[part], scale[1 - part]])[None, :, None]

    def step(index, carry):
        source = sources_of(blocks, index, chunk, parts, cluster)
        shape = source.shape[:-1]
        height = chunk * rows
        density = (source * target[None, :, None]).astype(BF16).reshape(height, PLANE)
        section = jnp.concatenate(
            [
                dot(x_table, density[at : at + group]).astype(BF16)
                for at in range(0, height, group)
            ]
        )
        section = dot(section, mix_y[...]).astype(BF16)
        spectrum = bands(section, z_table).reshape(shape + (WIDE,))
        section = (spectrum * factor).astype(BF16).reshape(height, WIDE)
        section = bands(section, z_table).astype(BF16)
        section = dot(section, mix_back[...]).astype(BF16)
        potential = jnp.concatenate(
            [dot(x_table, section[at : at + group]) for at in range(0, height, group)]
        ).reshape(shape + (PLANE,))
        weight = jnp.where(
            first,
            source[..., planes : planes + 1, :],
            source[..., stride + planes : stride + planes + 1, :],
        )
        totals[...] -= jnp.sum(weight * potential * source, axis=(0, 2))
        return carry

    steps = blocks.shape[0] // chunk
    if steps == 1:
        step(0, 0)
    else:
        lax.fori_loop(0, steps, step, 0)


def first_body(place, local, mix_x, mix_y, mix_z, mix_back, scale, totals, *, own, **sizes):
    target = target_of(place[1], local, own, sizes["stride"], sizes["cluster"])
    totals[...] = jnp.zeros_like(totals)
    add_pairs(
        place[1], target, local, mix_x, mix_y, mix_z, mix_back, scale, totals, **sizes
    )


def second_body(
    place, local, other, mix_x, mix_y, mix_z, mix_back, scale, before, sent, kept, totals,
    *, own, owner_bits, **sizes,
):
    stride, planes = sizes["stride"], sizes["planes"]
    parts, cluster, chunk = sizes["parts"], sizes["cluster"], sizes["chunk"]
    target = target_of(place[1], local, own, stride, cluster)
    totals[...] = before[...]
    add_pairs(
        place[1], target, other, mix_x, mix_y, mix_z, mix_back, scale, totals, **sizes
    )
    partial = totals[...]
    folded = partial + halves(partial, stride)
    rows = own * stride
    count = chunk // parts
    half = local.shape[0] // parts
    norb = 2 * half * own
    lane = lax.broadcasted_iota(jnp.int32, (count, norb), 1)
    slot = lax.broadcasted_iota(jnp.int32, (count, norb), 0)
    first = lax.broadcasted_iota(jnp.int32, (count, rows, PLANE), 1) < stride

    def overlap(blocks, base):
        def step(index, line):
            source = sources_of(blocks, index, chunk, parts, cluster)
            product = jnp.sum(source * folded[None, :, None], axis=1).reshape(count, rows, PLANE)
            owner = spell(base + index * count + slot, owner_bits) ^ place[0]
            for orbital in range(own):
                wanted = first if orbital == 0 else jnp.logical_not(first)
                picked = jnp.sum(jnp.where(wanted, product, 0.0), axis=1)
                value = jnp.sum(picked, axis=1, keepdims=True) / NPTS
                at = owner * own + orbital
                line = line + jnp.sum(jnp.where(lane == at, value, 0.0), axis=0, keepdims=True)
            return line

        return step

    line = jnp.zeros((1, norb), F32)
    steps = local.shape[0] // chunk
    for blocks, base in ((local, 0), (other, half)):
        step = overlap(blocks, base)
        line = step(0, line) if steps == 1 else lax.fori_loop(0, steps, step, line)
    line = jnp.concatenate([line, jnp.zeros((1, PLANE - norb), F32)], axis=1)
    high = line.astype(BF16).astype(F32)
    middle = (line - high).astype(BF16).astype(F32)
    low = line - high - middle
    height = sent.shape[1]
    row = lax.broadcasted_iota(jnp.int32, (1, height, PLANE), 1)
    mixed = folded[:, :height]
    for at, value in enumerate((high, middle, low)):
        mixed = jnp.where(row == planes + at, value[None], mixed)
    sent[...] = mixed.astype(BF16)
    kept[...] = folded[:, :height]


def solve_body(
    place, local, other, kept, partner, potentials, projectors, lines, work, weights,
    *, own, planes, bits, cluster,
):
    norb = lines.shape[0]
    half = norb // 2
    me = place[2]
    for blocks, base in ((local, 0), (other, half)):
        raw = blocks[:, :, :norb].astype(F32)
        lines[base : base + half] = (
            raw[:, planes] + raw[:, planes + 1] + raw[:, planes + 2]
        )

    def repeat(step):
        if norb <= 32:
            for at in range(norb):
                step(at)
        else:
            lax.fori_loop(0, norb, lambda at, carry: (step(at), carry)[1], 0)

    def settle(at):
        work[0, pl.ds(spell(at, bits) ^ me, 1), :] = lines[pl.ds(at, 1), :]

    repeat(settle)
    gram = work[0]
    left = -0.5 * (gram + gram.T)
    row = lax.broadcasted_iota(jnp.int32, (norb, norb), 0)
    column = lax.broadcasted_iota(jnp.int32, (norb, norb), 1)
    right = jnp.where(row == column, 1.0, 0.0).astype(F32)
    if norb <= 32:
        for k in range(norb):
            factor = jnp.where(row[:, :1] > k, left[:, k : k + 1] / left[k : k + 1, k : k + 1], 0.0)
            left, right = left - factor * left[k : k + 1], right - factor * right[k : k + 1]
    else:
        work[0] = left
        work[1] = right

        def step(k, carry):
            left = work[0]
            pivot_row = work[0, pl.ds(k, 1), :]
            right_row = work[1, pl.ds(k, 1), :]
            pivot = jnp.sum(jnp.where(column[:1] == k, pivot_row, 0.0), axis=1, keepdims=True)
            below = jnp.sum(jnp.where(column == k, left, 0.0), axis=1, keepdims=True)
            factor = jnp.where(row[:, :1] > k, below / pivot, 0.0)
            work[0] = left - factor * pivot_row
            work[1] = work[1] - factor * right_row
            return carry

        lax.fori_loop(0, norb, step, 0)
        left = work[0]
        right = work[1]
    diagonal = jnp.sum(jnp.where(row == column, left, 0.0), axis=1, keepdims=True)
    turned = (right * lax.rsqrt(diagonal)).T
    for orbital in range(own):
        at = place[0] * own + orbital
        value = jnp.sum(jnp.where(column == at, turned, 0.0), axis=1, keepdims=True)
        weights[orbital] = jnp.broadcast_to(value, (norb, PLANE))

    height = local.shape[1]
    own_values = kept[0]
    partner_values = partner[...]
    start = []
    for orbital in range(own):
        start.append(
            weights[orbital, pl.ds(me, 1), :] * (own_values - local[0].astype(F32))
            + weights[orbital, pl.ds(me ^ 1, 1), :]
            * (partner_values - local[cluster].astype(F32))
        )

    def gather(blocks, base):
        def step(at, sums):
            value = blocks[at].astype(F32)
            where = spell(base + at, bits) ^ me
            return tuple(
                sums[orbital] + weights[orbital, pl.ds(where, 1), :] * value
                for orbital in range(own)
            )

        return step

    sums = tuple(start)
    for blocks, base in ((local, 0), (other, half)):
        step = gather(blocks, base)
        if norb <= 32:
            for at in range(half):
                sums = step(at, sums)
        else:
            sums = lax.fori_loop(0, half, step, sums)
    second = place[1] == 1
    for orbital in range(own):
        swapped = second if orbital == 0 else jnp.logical_not(second)
        value = jnp.where(swapped, partner_values, own_values)
        for x in range(planes):
            lanes = slice(x * PLANE, (x + 1) * PLANE)
            potentials[orbital : orbital + 1, lanes] = value[x : x + 1]
            projectors[orbital : orbital + 1, lanes] = sums[orbital][x : x + 1]


def on_device(orbitals, occupation):
    own = orbitals.shape[0]
    owners = lax.axis_size("orb")
    parts = lax.axis_size("grid")
    devices = owners * parts
    planes = NX // parts
    stride = row_stride(own, planes)
    rows = own * stride
    route = Route(devices)
    cluster = route.cluster
    sizes = dict(parts=parts, stride=stride, planes=planes, cluster=cluster, chunk=16)
    orb, grid = lax.axis_index("orb"), lax.axis_index("grid")
    place = jnp.stack([orb, grid, orb * parts + grid]).astype(jnp.int32)
    vmem = pl.BlockSpec(memory_space=pltpu.VMEM)
    smem = pl.BlockSpec(memory_space=pltpu.SMEM)
    shape = jax.ShapeDtypeStruct
    mixing = [jnp.asarray(item) for item in tables(own, parts, cluster)]

    local = pl.pallas_call(
        functools.partial(pack_body, own=own, planes=planes, stride=stride),
        out_shape=shape((1, rows, PLANE), BF16),
        in_specs=[vmem, vmem],
        out_specs=vmem,
        name="pack",
    )(orbitals, occupation.reshape(own, 1))
    for members in route.rounds[:-1]:
        local = jnp.concatenate(
            [local] + [route.swap(local, mask) for mask in route.masks(members)[1:]]
        )
    other = route.swap(local, route.masks(route.rounds[-1])[1])

    totals_shape = (parts, rows, PLANE)
    before = pl.pallas_call(
        functools.partial(first_body, own=own, **sizes),
        out_shape=shape(totals_shape, F32),
        in_specs=[smem] + [vmem] * 6,
        out_specs=vmem,
        name="near_pairs",
    )(place, local, *mixing)
    height = 16
    sent, kept = pl.pallas_call(
        functools.partial(second_body, own=own, owner_bits=route.owner_bits, **sizes),
        out_shape=(shape((parts, height, PLANE), BF16), shape((parts, height, PLANE), F32)),
        in_specs=[smem] + [vmem] * 8,
        out_specs=(vmem, vmem),
        scratch_shapes=[pltpu.VMEM(totals_shape, F32)],
        name="far_pairs",
    )(place, local, other, *mixing, before)

    column = sent[:, None]
    column = jnp.concatenate(
        [column] + [route.swap(column, mask) for mask in route.masks(route.rounds[0])[1:]], axis=1
    )
    partner = route.swap(kept[1], 1)
    near, far = column[0], column[1]
    near = jnp.concatenate(
        [near]
        + [route.swap(far if mask & 1 else near, mask) for mask in route.masks(route.rounds[1])[1:]]
    )
    for members in route.rounds[2:-1]:
        near = jnp.concatenate(
            [near] + [route.swap(near, mask) for mask in route.masks(members)[1:]]
        )
    away = route.swap(near, route.masks(route.rounds[-1])[1])
    norb = devices
    size = planes * PLANE
    return tuple(
        pl.pallas_call(
            functools.partial(
                solve_body, own=own, planes=planes, bits=route.bits, cluster=cluster
            ),
            out_shape=(shape((own, size), F32), shape((own, size), F32)),
            in_specs=[smem] + [vmem] * 4,
            out_specs=(vmem, vmem),
            scratch_shapes=[
                pltpu.VMEM((norb, norb), F32),
                pltpu.VMEM((2, norb, norb), F32),
                pltpu.VMEM((own, norb, PLANE), F32),
            ],
            name="solve",
        )(place, near, away, kept, partner)
    )


def solution(mesh):
    placed = (P("orb", "grid"), P("orb"))
    return jax.shard_map(
        on_device,
        mesh=mesh,
        in_specs=placed,
        out_specs=(P("orb", "grid"), P("orb", "grid")),
        check_vma=False,
    )
```

time: 88.2 us -> 59.9 us (0.68)
  blocking collectives: 35.9 us -> 0 us
  starting transfers between devices: 7.33 us -> 18.8 us
  waiting for transfers between devices: 24.1 us -> 18.6 us
  Pallas kernels: 11.6 us -> 15.4 us
  local copies, waits for them, and re-layouts: 6.81 us -> 4.39 us
    all_to_all x1 -> x0, blocking collectives: 35.9 us -> none  [spread(): lax.all_to_all(blocks, ('orb', 'grid'), split_axis=0, concat_axis=0, tile...]
    all_to_all x1 -> x0, waiting for transfers between devices: 24.1 us -> none  [spread(): lax.all_to_all(blocks, ('orb', 'grid'), split_axis=0, concat_axis=0, tile...]
    ppermute x0 -> x15, starting transfers between devices: none -> 18.8 us  [swap(): return lax.ppermute(array, ('orb', 'grid'), pairs)]
    ppermute x0 -> x15, waiting for transfers between devices: none -> 18.6 us  [swap(): return lax.ppermute(array, ('orb', 'grid'), pairs)]
    all_to_all x1 -> x0, starting transfers between devices: 7.33 us -> none  [spread(): lax.all_to_all(blocks, ('orb', 'grid'), split_axis=0, concat_axis=0, tile...]
    pallas_call x2 -> x4, Pallas kernels: 11.6 us -> 15.4 us  [the longest x1 5.09 us: on_device(): pl.pallas_call(functools.partial(solve_body, own=own, planes=planes, bits...]
    reshape x3 -> x1, local copies, waits for them, and re-layouts: 4.05 us -> 0.61 us  [on_device(): occupation.reshape(own, 1)]
    unnamed x2 -> x22, local copies, waits for them, and re-layouts: 0.97 us -> 3.74 us
  transfers between devices with their start and end apart: 1 -> 15, of which waited for: 1 -> 12; matrix products, arithmetic and copies ran while one was open for 1% -> 3% of each run, Pallas kernels for 0% -> 7%
where the time goes in v2:
time: 59.9 us; the launch traced here: 59.4 us
  starting transfers between devices  18.8 us (31%)
  waiting for transfers between devices  18.6 us (31%)
  Pallas kernels  15.4 us (26%)
  local copies, waits for them, and re-layouts  4.39 us (7%)
  other arithmetic  1.54 us (3%)
  between operations  0.74 us (1%)
    ppermute x15, starting transfers between devices, swap(): return lax.ppermute(array, ('orb', 'grid'), pairs)  18.8 us
    ppermute x15, waiting for transfers between devices, swap(): return lax.ppermute(array, ('orb', 'grid'), pairs)  18.6 us
    pallas_call x1, Pallas kernels, on_device(): pl.pallas_call(functools.partial(solve_body, own=own, planes=planes, bits...  5.09 us
    pallas_call x1, Pallas kernels, on_device(): pl.pallas_call(functools.partial(second_body, own=own, owner_bits=route.o...  4.7 us
    pallas_call x1, Pallas kernels, on_device(): pl.pallas_call(functools.partial(first_body, own=own, **sizes), out_shape...  4.13 us
    unnamed x22, local copies, waits for them, and re-layouts  3.74 us
    pallas_call x1, Pallas kernels, on_device(): pl.pallas_call(functools.partial(pack_body, own=own, planes=planes, strid...  1.45 us
  transfers between devices with their start and end apart: 15, of which 12 were waited for; matrix products, arithmetic and copies ran while one was open for 3% of the time, Pallas kernels for 7%

profile of v2, /device:TPU:0, one launch (start us, length us, event | category | flops | bytes accessed | tf_op | source)
XLA Modules:
  0.0 59.4 jit_solution(15796402775583494500)
XLA Ops:
  0.6 0.0 copy-start.7
  0.6 0.6 %copy-done.7 = bf16[2]{0:T(256)(128)(2,1)S(1)} copy-done((bf16[2]{0:T(256)(128)(2,1)S(1)}, bf16[2]{0:T(256)(128)(2,1)}, u32[]{:S(2)}) %copy-start.7) | copy-done | bytes 28
  1.3 0.6 %copy.9.occupation = bf16[2,1]{1,0:T(2,128)(2,1)} copy(bf16[2,1]{0,1:T(2,128)(2,1)S(1)} %bitcast.15) | data formatting | bytes 8 | tf_op jit(solution)/shard_map/reshape | solution.py:387
  1.9 1.5 %pack.1 = bf16[1,24,576]{2,1,0:T(8,128)(2,1)} custom-call(bf16[2,5760]{1,0:T(2,128)(2,1)} %orbitals.1, bf16[2,1]{1,0:T(2,128)(2,1)} %copy.9.occupation), custom_call_target="tpu_custom_call" | custom-call | tf_op jit(solution)/shard_map/pack/pallas_call | solution.py:381
  3.3 0.0 copy-start.4
  3.4 3.1 %collective-permute-start = (bf16[1,24,576]{2,1,0:T(8,128)(2,1)}, bf16[1,24,576]{2,1,0:T(8,128)(2,1)S(1)}, u32[]{:S(2)}, u32[]{:S(2)}) collective-permute-start(bf16[1,24,576]{2,1,0:T(8,128)(2,1)} %pack.1), channel_id=1, source_target_pairs={{0,8},{1,9},{2,10},{3,11},{4,12},{5,13},{6,14},{7,15},{8,0},{9,1},... | collective-permute-start | bytes 82952 | tf_op jit(solution)/shard_map/ppermute | solution.py:127
  6.4 2.6 %collective-permute-start.1 = (bf16[1,24,576]{2,1,0:T(8,128)(2,1)}, bf16[1,24,576]{2,1,0:T(8,128)(2,1)S(1)}, u32[]{:S(2)}, u32[]{:S(2)}) collective-permute-start(bf16[1,24,576]{2,1,0:T(8,128)(2,1)} %pack.1), channel_id=1, source_target_pairs={{0,16},{1,17},{2,18},{3,19},{4,20},{5,21},{6,22},{7,23},{8,24},{9,... | collective-permute-start | bytes 82952 | tf_op jit(solution)/shard_map/ppermute | solution.py:127
  9.0 0.0 collective-permute-start.2
  9.0 0.8 %constant_dynamic-update-slice_fusion.6 = bf16[16,24,576]{2,1,0:T(8,128)(2,1)S(1)} fusion(bf16[1,24,576]{2,1,0:T(8,128)(2,1)} %pack.1), kind=kLoop, calls=%fused_computation.12 | loop fusion | bytes 58368
  9.8 0.0 collective-permute-done
  9.8 2.1 %collective-permute-done.1 = bf16[1,24,576]{2,1,0:T(8,128)(2,1)S(1)} collective-permute-done((bf16[1,24,576]{2,1,0:T(8,128)(2,1)}, bf16[1,24,576]{2,1,0:T(8,128)(2,1)S(1)}, u32[]{:S(2)}, u32[]{:S(2)}) %collective-permute-start.1) | collective-permute-done | bytes 27680 | tf_op jit(solution)/shard_map/ppermute | solution.py:127
  11.9 3.0 %collective-permute-done.2 = bf16[1,24,576]{2,1,0:T(8,128)(2,1)S(1)} collective-permute-done((bf16[1,24,576]{2,1,0:T(8,128)(2,1)}, bf16[1,24,576]{2,1,0:T(8,128)(2,1)S(1)}, u32[]{:S(2)}, u32[]{:S(2)}) %collective-permute-start.2) | collective-permute-done | bytes 27680 | tf_op jit(solution)/shard_map/ppermute | solution.py:127
  14.9 0.0 copy-done.4
  14.9 1.6 %collective-permute-start.3 = (bf16[4,24,576]{2,1,0:T(8,128)(2,1)S(1)}, bf16[4,24,576]{2,1,0:T(8,128)(2,1)S(1)}, u32[]{:S(2)}, u32[]{:S(2)}) collective-permute-start(bf16[4,24,576]{2,1,0:T(8,128)(2,1)S(1)} %pad_maximum_fusion.2), channel_id=1, source_target_pairs={{0,1},{1,0},{2,3},{3,2},{4,5},{5,4},{6,7},{7,6},{8,9},{9,8},{10,11... | collective-permute-start | bytes 331784 | tf_op jit(solution)/shard_map/ppermute | solution.py:127
  16.5 1.5 %collective-permute-start.4 = (bf16[4,24,576]{2,1,0:T(8,128)(2,1)S(1)}, bf16[4,24,576]{2,1,0:T(8,128)(2,1)S(1)}, u32[]{:S(2)}, u32[]{:S(2)}) collective-permute-start(bf16[4,24,576]{2,1,0:T(8,128)(2,1)S(1)} %pad_maximum_fusion.2), channel_id=1, source_target_pairs={{0,4},{1,5},{2,6},{3,7},{4,0},{5,1},{6,2},{7,3},{8,12},{9,13},{10,... | collective-permute-start | bytes 331784 | tf_op jit(solution)/shard_map/ppermute | solution.py:127
  18.0 0.5 collective-permute-start.5
  18.5 2.3 %collective-permute-done.3 = bf16[4,24,576]{2,1,0:T(8,128)(2,1)S(1)} collective-permute-done((bf16[4,24,576]{2,1,0:T(8,128)(2,1)S(1)}, bf16[4,24,576]{2,1,0:T(8,128)(2,1)S(1)}, u32[]{:S(2)}, u32[]{:S(2)}) %collective-permute-start.3) | collective-permute-done | bytes 110624 | tf_op jit(solution)/shard_map/ppermute | solution.py:127
  20.9 1.2 %collective-permute-done.4 = bf16[4,24,576]{2,1,0:T(8,128)(2,1)S(1)} collective-permute-done((bf16[4,24,576]{2,1,0:T(8,128)(2,1)S(1)}, bf16[4,24,576]{2,1,0:T(8,128)(2,1)S(1)}, u32[]{:S(2)}, u32[]{:S(2)}) %collective-permute-start.4) | collective-permute-done | bytes 110624 | tf_op jit(solution)/shard_map/ppermute | solution.py:127
  22.1 1.7 %collective-permute-done.5 = bf16[4,24,576]{2,1,0:T(8,128)(2,1)S(1)} collective-permute-done((bf16[4,24,576]{2,1,0:T(8,128)(2,1)S(1)}, bf16[4,24,576]{2,1,0:T(8,128)(2,1)S(1)}, u32[]{:S(2)}, u32[]{:S(2)}) %collective-permute-start.5) | collective-permute-done | bytes 110624 | tf_op jit(solution)/shard_map/ppermute | solution.py:127
  23.8 0.0 copy-start
  23.8 0.1 collective-permute-start.6
  23.9 0.6 %pad_add_fusion.place = s32[3]{0:T(128)} fusion(s32[1]{0:T(128)} %bitcast.2, s32[1]{0:T(128)} %bitcast.1, s32[1]{0:T(128)} %bitcast), kind=kLoop, calls=%fused_computation.13 | loop fusion | flops 6 | bytes 24 | tf_op jit(solution)/shard_map/stack | solution.py:375
  24.5 0.1 copy-done
  24.6 4.1 %near_pairs.1.before = f32[2,24,576]{2,1,0:T(8,128)} custom-call(s32[3]{0:T(128)} %pad_add_fusion.place, bf16[16,24,576]{2,1,0:T(8,128)(2,1)} %copy-done, bf16[2,192,192]{2,1,0:T(8,128)(2,1)} %constant.20.clone.mix_x, bf16[576,640]{1,0:T(8,128)(2,1)} %constant.21.clone.mix_y, bf16[256,256]{1,0:T(8,128)(2,1)} %constant.22.clone.mix_z, ...), custom_call_target="tpu_custom_call" | custom-call | tf_op jit(solution)/shard_map/near_pairs/pallas_call | solution.py:395
  28.7 0.0 collective-permute-done.6.other
  28.7 0.0 copy-start.2
  28.7 0.8 %copy-done.2 = bf16[16,24,576]{2,1,0:T(8,128)(2,1)} copy-done((bf16[16,24,576]{2,1,0:T(8,128)(2,1)}, bf16[16,24,576]{2,1,0:T(8,128)(2,1)S(1)}, u32[]{:S(2)}) %copy-start.2) | copy-done | bytes 442392
  29.5 4.7 %far_pairs.1 = (bf16[2,16,576]{2,1,0:T(8,128)(2,1)}, f32[2,16,576]{2,1,0:T(8,128)}) custom-call(s32[3]{0:T(128)} %pad_add_fusion.place, bf16[16,24,576]{2,1,0:T(8,128)(2,1)} %copy-done, bf16[16,24,576]{2,1,0:T(8,128)(2,1)} %copy-done.2, bf16[2,192,192]{2,1,0:T(8,128)(2,1)} %constant.20.clone.mix_x, bf16[576,640]{1,0:T(8,128)(2,1)} %constant.21.clone.mix_y, ...), custom_call_target="tpu_custom_call" | custom-call | tf_op jit(solution)/shard_map/far_pairs/pallas_call | solution.py:403
  34.2 0.3 collective-permute-start.9
  34.6 0.1 collective-permute-start.8
  34.7 3.9 %collective-permute-start.7 = (bf16[2,1,16,576]{3,2,1,0:T(8,128)(2,1)}, bf16[2,1,16,576]{3,2,1,0:T(8,128)(2,1)S(1)}, u32[]{:S(2)}, u32[]{:S(2)}) collective-permute-start(bf16[2,1,16,576]{3,2,1,0:T(8,128)(2,1)} %bitcast.13), channel_id=1, source_target_pairs={{0,8},{1,9},{2,10},{3,11},{4,12},{5,13},{6,14},{7,15},{8,0},{9,1},... | collective-permute-start | bytes 110600 | tf_op jit(solution)/shard_map/ppermute | solution.py:127
  38.6 2.1 %collective-permute-done.9 = bf16[2,1,16,576]{3,2,1,0:T(8,128)(2,1)S(1)} collective-permute-done((bf16[2,1,16,576]{3,2,1,0:T(8,128)(2,1)}, bf16[2,1,16,576]{3,2,1,0:T(8,128)(2,1)S(1)}, u32[]{:S(2)}, u32[]{:S(2)}) %collective-permute-start.9) | collective-permute-done | bytes 36896 | tf_op jit(solution)/shard_map/ppermute | solution.py:127
  40.7 0.6 %collective-permute-done.8 = bf16[2,1,16,576]{3,2,1,0:T(8,128)(2,1)S(1)} collective-permute-done((bf16[2,1,16,576]{3,2,1,0:T(8,128)(2,1)}, bf16[2,1,16,576]{3,2,1,0:T(8,128)(2,1)S(1)}, u32[]{:S(2)}, u32[]{:S(2)}) %collective-permute-start.8) | collective-permute-done | bytes 36896 | tf_op jit(solution)/shard_map/ppermute | solution.py:127
  41.3 0.1 collective-permute-done.7
  41.4 0.8 %pad_maximum_fusion.1 = bf16[2,4,16,576]{3,2,1,0:T(8,128)(2,1)S(1)} fusion(bf16[2,1,16,576]{3,2,1,0:T(8,128)(2,1)S(1)} %collective-permute-done.9, bf16[2,1,16,576]{3,2,1,0:T(8,128)(2,1)S(1)} %collective-permute-done.8, bf16[2,1,16,576]{3,2,1,0:T(8,128)(2,1)S(1)} %collective-permute-done.7, bf16[2,1,16,576]{3,2,1,0:T(8,128)(2,1)} %bitcast.14), kind=kLoop, calls=%fused_computation.1 | loop fusion | flops 221184 | bytes 294912 | tf_op jit(solution)/shard_map/concatenate | solution.py:413
  42.3 0.5 collective-permute-start.12
  42.8 0.0 copy-start.5
  42.8 1.5 %collective-permute-start.11 = (bf16[4,16,576]{2,1,0:T(8,128)(2,1)S(1)}, bf16[4,16,576]{2,1,0:T(8,128)(2,1)S(1)}, u32[]{:S(2)}, u32[]{:S(2)}) collective-permute-start(bf16[4,16,576]{2,1,0:T(8,128)(2,1)S(1)} %get-tuple-element.6), channel_id=1, source_target_pairs={{0,4},{1,5},{2,6},{3,7},{4,0},{5,1},{6,2},{7,3},{8,12},{9,13},{10,... | collective-permute-start | bytes 221192 | tf_op jit(solution)/shard_map/ppermute | solution.py:127
  44.3 1.5 %collective-permute-start.10 = (bf16[4,16,576]{2,1,0:T(8,128)(2,1)S(1)}, bf16[4,16,576]{2,1,0:T(8,128)(2,1)S(1)}, u32[]{:S(2)}, u32[]{:S(2)}) collective-permute-start(bf16[4,16,576]{2,1,0:T(8,128)(2,1)S(1)} %get-tuple-element.7), channel_id=1, source_target_pairs={{0,1},{1,0},{2,3},{3,2},{4,5},{5,4},{6,7},{7,6},{8,9},{9,8},{10,11... | collective-permute-start | bytes 221192 | tf_op jit(solution)/shard_map/ppermute | solution.py:127
  45.8 2.2 %collective-permute-done.12 = bf16[4,16,576]{2,1,0:T(8,128)(2,1)S(1)} collective-permute-done((bf16[4,16,576]{2,1,0:T(8,128)(2,1)S(1)}, bf16[4,16,576]{2,1,0:T(8,128)(2,1)S(1)}, u32[]{:S(2)}, u32[]{:S(2)}) %collective-permute-start.12) | collective-permute-done | bytes 73760 | tf_op jit(solution)/shard_map/ppermute | solution.py:127
  48.0 0.1 collective-permute-done.11
  48.2 0.6 %collective-permute-done.10 = bf16[4,16,576]{2,1,0:T(8,128)(2,1)S(1)} collective-permute-done((bf16[4,16,576]{2,1,0:T(8,128)(2,1)S(1)}, bf16[4,16,576]{2,1,0:T(8,128)(2,1)S(1)}, u32[]{:S(2)}, u32[]{:S(2)}) %collective-permute-start.10) | collective-permute-done | bytes 73760 | tf_op jit(solution)/shard_map/ppermute | solution.py:127
  48.8 0.1 pad_maximum_fusion.local
  48.8 0.0 copy-start.1
  48.8 0.1 collective-permute-start.13
  48.9 0.0 copy-done.5
  48.9 1.6 %collective-permute-start.14 = (f32[16,576]{1,0:T(8,128)S(1)}, f32[16,576]{1,0:T(8,128)S(1)}, u32[]{:S(2)}, u32[]{:S(2)}) collective-permute-start(f32[16,576]{1,0:T(8,128)S(1)} %slice_bitcast_fusion.2), channel_id=1, source_target_pairs={{0,1},{1,0},{2,3},{3,2},{4,5},{5,4},{6,7},{7,6},{8,9},{9,8},{10,11... | collective-permute-start | bytes 110600 | tf_op jit(solution)/shard_map/ppermute | solution.py:127
  50.5 2.5 %collective-permute-done.14.partner = f32[16,576]{1,0:T(8,128)S(1)} collective-permute-done((f32[16,576]{1,0:T(8,128)S(1)}, f32[16,576]{1,0:T(8,128)S(1)}, u32[]{:S(2)}, u32[]{:S(2)}) %collective-permute-start.14) | collective-permute-done | bytes 36896 | tf_op jit(solution)/shard_map/ppermute | solution.py:127
  53.0 0.0 copy-start.6
  53.0 0.0 collective-permute-done.13.other
  53.0 0.0 copy-done.1
  53.0 0.6 %copy-done.6 = f32[16,576]{1,0:T(8,128)} copy-done((f32[16,576]{1,0:T(8,128)}, f32[16,576]{1,0:T(8,128)S(1)}, u32[]{:S(2)}) %copy-start.6) | copy-done | bytes 36888
  53.6 0.0 copy-start.3
  53.6 0.7 %copy-done.3 = bf16[16,16,576]{2,1,0:T(8,128)(2,1)} copy-done((bf16[16,16,576]{2,1,0:T(8,128)(2,1)}, bf16[16,16,576]{2,1,0:T(8,128)(2,1)S(1)}, u32[]{:S(2)}) %copy-start.3) | copy-done | bytes 294936
  54.4 5.1 %solve.1 = (f32[2,5760]{1,0:T(2,128)}, f32[2,5760]{1,0:T(2,128)}) custom-call(s32[3]{0:T(128)} %pad_add_fusion.place, bf16[16,16,576]{2,1,0:T(8,128)(2,1)} %copy-done.1, bf16[16,16,576]{2,1,0:T(8,128)(2,1)} %copy-done.3, f32[2,16,576]{2,1,0:T(8,128)} %get-tuple-element.5.kept, f32[16,576]{1,0:T(8,128)} %copy-done.6), custom_call_target="tpu_custom_call" | custom-call | tf_op jit(solution)/shard_map/solve/pallas_call | solution.py:430
  (9 shorter events, 0.1 us)
Async XLA Ops:
  0.6 0.7 %copy-start.7 = (bf16[2]{0:T(256)(128)(2,1)S(1)}, bf16[2]{0:T(256)(128)(2,1)}, u32[]{:S(2)}) copy-start(bf16[2]{0:T(256)(128)(2,1)} %param.8) | copy-start | bytes 16
  3.3 11.5 %copy-start.4 = (bf16[1,24,576]{2,1,0:T(8,128)(2,1)S(1)}, bf16[1,24,576]{2,1,0:T(8,128)(2,1)}, u32[]{:S(2)}) copy-start(bf16[1,24,576]{2,1,0:T(8,128)(2,1)} %pack.1) | copy-start | bytes 82948
  3.4 6.5 %collective-permute-start = (bf16[1,24,576]{2,1,0:T(8,128)(2,1)}, bf16[1,24,576]{2,1,0:T(8,128)(2,1)S(1)}, u32[]{:S(2)}, u32[]{:S(2)}) collective-permute-start(bf16[1,24,576]{2,1,0:T(8,128)(2,1)} %pack.1), channel_id=1, source_target_pairs={{0,8},{1,9},{2,10},{3,11},{4,12},{5,13},{6,14},{7,15},{8,0},{9,1},... | collective-permute-start | bytes 82952 | tf_op jit(solution)/shard_map/ppermute | solution.py:127
  6.4 5.5 %collective-permute-start.1 = (bf16[1,24,576]{2,1,0:T(8,128)(2,1)}, bf16[1,24,576]{2,1,0:T(8,128)(2,1)S(1)}, u32[]{:S(2)}, u32[]{:S(2)}) collective-permute-start(bf16[1,24,576]{2,1,0:T(8,128)(2,1)} %pack.1), channel_id=1, source_target_pairs={{0,16},{1,17},{2,18},{3,19},{4,20},{5,21},{6,22},{7,23},{8,24},{9,... | collective-permute-start | bytes 82952 | tf_op jit(solution)/shard_map/ppermute | solution.py:127
  9.0 5.9 %collective-permute-start.2 = (bf16[1,24,576]{2,1,0:T(8,128)(2,1)}, bf16[1,24,576]{2,1,0:T(8,128)(2,1)S(1)}, u32[]{:S(2)}, u32[]{:S(2)}) collective-permute-start(bf16[1,24,576]{2,1,0:T(8,128)(2,1)} %pack.1), channel_id=1, source_target_pairs={{0,24},{1,25},{2,26},{3,27},{4,28},{5,29},{6,30},{7,31},{8,16},{9,... | collective-permute-start | bytes 82952 | tf_op jit(solution)/shard_map/ppermute | solution.py:127
  14.9 5.9 %collective-permute-start.3 = (bf16[4,24,576]{2,1,0:T(8,128)(2,1)S(1)}, bf16[4,24,576]{2,1,0:T(8,128)(2,1)S(1)}, u32[]{:S(2)}, u32[]{:S(2)}) collective-permute-start(bf16[4,24,576]{2,1,0:T(8,128)(2,1)S(1)} %pad_maximum_fusion.2), channel_id=1, source_target_pairs={{0,1},{1,0},{2,3},{3,2},{4,5},{5,4},{6,7},{7,6},{8,9},{9,8},{10,11... | collective-permute-start | bytes 331784 | tf_op jit(solution)/shard_map/ppermute | solution.py:127
  16.5 5.6 %collective-permute-start.4 = (bf16[4,24,576]{2,1,0:T(8,128)(2,1)S(1)}, bf16[4,24,576]{2,1,0:T(8,128)(2,1)S(1)}, u32[]{:S(2)}, u32[]{:S(2)}) collective-permute-start(bf16[4,24,576]{2,1,0:T(8,128)(2,1)S(1)} %pad_maximum_fusion.2), channel_id=1, source_target_pairs={{0,4},{1,5},{2,6},{3,7},{4,0},{5,1},{6,2},{7,3},{8,12},{9,13},{10,... | collective-permute-start | bytes 331784 | tf_op jit(solution)/shard_map/ppermute | solution.py:127
  18.0 5.8 %collective-permute-start.5 = (bf16[4,24,576]{2,1,0:T(8,128)(2,1)S(1)}, bf16[4,24,576]{2,1,0:T(8,128)(2,1)S(1)}, u32[]{:S(2)}, u32[]{:S(2)}) collective-permute-start(bf16[4,24,576]{2,1,0:T(8,128)(2,1)S(1)} %pad_maximum_fusion.2), channel_id=1, source_target_pairs={{0,5},{1,4},{2,7},{3,6},{4,1},{5,0},{6,3},{7,2},{8,13},{9,12},{10,... | collective-permute-start | bytes 331784 | tf_op jit(solution)/shard_map/ppermute | solution.py:127
  23.8 0.8 %copy-start = (bf16[16,24,576]{2,1,0:T(8,128)(2,1)}, bf16[16,24,576]{2,1,0:T(8,128)(2,1)S(1)}, u32[]{:S(2)}) copy-start(bf16[16,24,576]{2,1,0:T(8,128)(2,1)S(1)} %constant_dynamic-update-slice_fusion.local) | copy-start | bytes 1327108
  23.8 4.9 %collective-permute-start.6 = (bf16[16,24,576]{2,1,0:T(8,128)(2,1)S(1)}, bf16[16,24,576]{2,1,0:T(8,128)(2,1)S(1)}, u32[]{:S(2)}, u32[]{:S(2)}) collective-permute-start(bf16[16,24,576]{2,1,0:T(8,128)(2,1)S(1)} %constant_dynamic-update-slice_fusion.local), channel_id=1, source_target_pairs={{0,2},{1,3},{2,0},{3,1},{4,6},{5,7},{6,4},{7,5},{8,10},{9,11},{10,... | collective-permute-start | bytes 1327112 | tf_op jit(solution)/shard_map/ppermute | solution.py:127
  28.7 0.8 %copy-start.2 = (bf16[16,24,576]{2,1,0:T(8,128)(2,1)}, bf16[16,24,576]{2,1,0:T(8,128)(2,1)S(1)}, u32[]{:S(2)}) copy-start(bf16[16,24,576]{2,1,0:T(8,128)(2,1)S(1)} %collective-permute-done.6.other) | copy-start | bytes 1327108
  34.2 6.4 %collective-permute-start.9 = (bf16[2,1,16,576]{3,2,1,0:T(8,128)(2,1)}, bf16[2,1,16,576]{3,2,1,0:T(8,128)(2,1)S(1)}, u32[]{:S(2)}, u32[]{:S(2)}) collective-permute-start(bf16[2,1,16,576]{3,2,1,0:T(8,128)(2,1)} %bitcast.11), channel_id=1, source_target_pairs={{0,24},{1,25},{2,26},{3,27},{4,28},{5,29},{6,30},{7,31},{8,16},{9,... | collective-permute-start | bytes 110600 | tf_op jit(solution)/shard_map/ppermute | solution.py:127
  34.6 6.7 %collective-permute-start.8 = (bf16[2,1,16,576]{3,2,1,0:T(8,128)(2,1)}, bf16[2,1,16,576]{3,2,1,0:T(8,128)(2,1)S(1)}, u32[]{:S(2)}, u32[]{:S(2)}) collective-permute-start(bf16[2,1,16,576]{3,2,1,0:T(8,128)(2,1)} %bitcast.12), channel_id=1, source_target_pairs={{0,16},{1,17},{2,18},{3,19},{4,20},{5,21},{6,22},{7,23},{8,24},{9,... | collective-permute-start | bytes 110600 | tf_op jit(solution)/shard_map/ppermute | solution.py:127
  34.7 6.8 %collective-permute-start.7 = (bf16[2,1,16,576]{3,2,1,0:T(8,128)(2,1)}, bf16[2,1,16,576]{3,2,1,0:T(8,128)(2,1)S(1)}, u32[]{:S(2)}, u32[]{:S(2)}) collective-permute-start(bf16[2,1,16,576]{3,2,1,0:T(8,128)(2,1)} %bitcast.13), channel_id=1, source_target_pairs={{0,8},{1,9},{2,10},{3,11},{4,12},{5,13},{6,14},{7,15},{8,0},{9,1},... | collective-permute-start | bytes 110600 | tf_op jit(solution)/shard_map/ppermute | solution.py:127
  42.3 5.8 %collective-permute-start.12 = (bf16[4,16,576]{2,1,0:T(8,128)(2,1)S(1)}, bf16[4,16,576]{2,1,0:T(8,128)(2,1)S(1)}, u32[]{:S(2)}, u32[]{:S(2)}) collective-permute-start(bf16[4,16,576]{2,1,0:T(8,128)(2,1)S(1)} %get-tuple-element.7), channel_id=1, source_target_pairs={{0,5},{1,4},{2,7},{3,6},{4,1},{5,0},{6,3},{7,2},{8,13},{9,12},{10,... | collective-permute-start | bytes 221192 | tf_op jit(solution)/shard_map/ppermute | solution.py:127
  42.8 6.1 %copy-start.5 = (f32[2,16,576]{2,1,0:T(8,128)S(1)}, f32[2,16,576]{2,1,0:T(8,128)}, u32[]{:S(2)}) copy-start(f32[2,16,576]{2,1,0:T(8,128)} %get-tuple-element.5.kept) | copy-start | bytes 221188
  42.8 5.4 %collective-permute-start.11 = (bf16[4,16,576]{2,1,0:T(8,128)(2,1)S(1)}, bf16[4,16,576]{2,1,0:T(8,128)(2,1)S(1)}, u32[]{:S(2)}, u32[]{:S(2)}) collective-permute-start(bf16[4,16,576]{2,1,0:T(8,128)(2,1)S(1)} %get-tuple-element.6), channel_id=1, source_target_pairs={{0,4},{1,5},{2,6},{3,7},{4,0},{5,1},{6,2},{7,3},{8,12},{9,13},{10,... | collective-permute-start | bytes 221192 | tf_op jit(solution)/shard_map/ppermute | solution.py:127
  44.3 4.4 %collective-permute-start.10 = (bf16[4,16,576]{2,1,0:T(8,128)(2,1)S(1)}, bf16[4,16,576]{2,1,0:T(8,128)(2,1)S(1)}, u32[]{:S(2)}, u32[]{:S(2)}) collective-permute-start(bf16[4,16,576]{2,1,0:T(8,128)(2,1)S(1)} %get-tuple-element.7), channel_id=1, source_target_pairs={{0,1},{1,0},{2,3},{3,2},{4,5},{5,4},{6,7},{7,6},{8,9},{9,8},{10,11... | collective-permute-start | bytes 221192 | tf_op jit(solution)/shard_map/ppermute | solution.py:127
  48.8 4.2 %copy-start.1 = (bf16[16,16,576]{2,1,0:T(8,128)(2,1)}, bf16[16,16,576]{2,1,0:T(8,128)(2,1)S(1)}, u32[]{:S(2)}) copy-start(bf16[16,16,576]{2,1,0:T(8,128)(2,1)S(1)} %pad_maximum_fusion.local) | copy-start | bytes 884740
  48.8 4.2 %collective-permute-start.13 = (bf16[16,16,576]{2,1,0:T(8,128)(2,1)S(1)}, bf16[16,16,576]{2,1,0:T(8,128)(2,1)S(1)}, u32[]{:S(2)}, u32[]{:S(2)}) collective-permute-start(bf16[16,16,576]{2,1,0:T(8,128)(2,1)S(1)} %pad_maximum_fusion.local), channel_id=1, source_target_pairs={{0,2},{1,3},{2,0},{3,1},{4,6},{5,7},{6,4},{7,5},{8,10},{9,11},{10,... | collective-permute-start | bytes 884744 | tf_op jit(solution)/shard_map/ppermute | solution.py:127
  48.9 4.1 %collective-permute-start.14 = (f32[16,576]{1,0:T(8,128)S(1)}, f32[16,576]{1,0:T(8,128)S(1)}, u32[]{:S(2)}, u32[]{:S(2)}) collective-permute-start(f32[16,576]{1,0:T(8,128)S(1)} %slice_bitcast_fusion.2), channel_id=1, source_target_pairs={{0,1},{1,0},{2,3},{3,2},{4,5},{5,4},{6,7},{7,6},{8,9},{9,8},{10,11... | collective-permute-start | bytes 110600 | tf_op jit(solution)/shard_map/ppermute | solution.py:127
  53.0 0.6 %copy-start.6 = (f32[16,576]{1,0:T(8,128)}, f32[16,576]{1,0:T(8,128)S(1)}, u32[]{:S(2)}) copy-start(f32[16,576]{1,0:T(8,128)S(1)} %collective-permute-done.14.partner) | copy-start | bytes 110596
  53.6 0.7 %copy-start.3 = (bf16[16,16,576]{2,1,0:T(8,128)(2,1)}, bf16[16,16,576]{2,1,0:T(8,128)(2,1)S(1)}, u32[]{:S(2)}) copy-start(bf16[16,16,576]{2,1,0:T(8,128)(2,1)S(1)} %collective-permute-done.13.other) | copy-start | bytes 884740

commit v3 on v2

--- a/solution.py
+++ b/solution.py
@@ -107,7 +107,7 @@
     def __init__(self, devices):
         top = devices.bit_length() - 1
         rest = list(range(top - 1, 1, -1))
-        rounds = [rest[:2], rest[2:3] + [0]]
+        rounds = [rest[:2][::-1], rest[2:3] + [0]]
         rounds += [rest[at : at + 2] for at in range(3, len(rest), 2)] + [[1]]
         self.devices = devices
         self.rounds = rounds
@@ -385,7 +385,9 @@
         out_specs=vmem,
         name="pack",
     )(orbitals, occupation.reshape(own, 1))
-    for members in route.rounds[:-1]:
+    for bit in reversed(route.rounds[0]):
+        local = jnp.concatenate([local, route.swap(local, 1 << bit)])
+    for members in route.rounds[1:-1]:
         local = jnp.concatenate(
             [local] + [route.swap(local, mask) for mask in route.masks(members)[1:]]
         )
@@ -414,6 +416,7 @@
         [column] + [route.swap(column, mask) for mask in route.masks(route.rounds[0])[1:]], axis=1
     )
     partner = route.swap(kept[1], 1)
+    column, partner = lax.optimization_barrier((column, partner))
     near, far = column[0], column[1]
     near = jnp.concatenate(
         [near]

time: 59.9 us -> 57.9 us (0.967)
  starting transfers between devices: 18.8 us -> 17.7 us
  waiting for transfers between devices: 18.6 us -> 17.8 us
  other arithmetic: 1.54 us -> 0.79 us
  local copies, waits for them, and re-layouts: 4.39 us -> 5.1 us
    ppermute x15 -> x14, starting transfers between devices: 18.8 us -> 17.7 us  [swap(): return lax.ppermute(array, ('orb', 'grid'), pairs)]
    squeeze x1, local copies, waits for them, and re-layouts: 0.01 us -> 0.79 us  [on_device(): partner = route.swap(kept[1], 1)]
    ppermute x15 -> x14, waiting for transfers between devices: 18.6 us -> 17.8 us  [swap(): return lax.ppermute(array, ('orb', 'grid'), pairs)]
    concatenate x1, other arithmetic: 0.81 us -> 0.03 us  [on_device(): jnp.concatenate([column] + [route.swap(column, mask) for mask in route.ma...]
    unnamed x22 -> x21, local copies, waits for them, and re-layouts: 3.74 us -> 3.67 us
  transfers between devices with their start and end apart: 15 -> 14, of which waited for: 12 -> 13; matrix products, arithmetic and copies ran while one was open for 3% -> 4% of each run, Pallas kernels for 7% -> 7%
where the time goes in v3:
time: 57.9 us; the launch traced here: 57.5 us
  waiting for transfers between devices  17.8 us (31%)
  starting transfers between devices  17.7 us (31%)
  Pallas kernels  15.4 us (27%)
  local copies, waits for them, and re-layouts  5.1 us (9%)
  other arithmetic  0.79 us (1%)
  between operations  0.72 us (1%)
    ppermute x14, waiting for transfers between devices, swap(): return lax.ppermute(array, ('orb', 'grid'), pairs)  17.8 us
    ppermute x14, starting transfers between devices, swap(): return lax.ppermute(array, ('orb', 'grid'), pairs)  17.7 us
    pallas_call x1, Pallas kernels, on_device(): pl.pallas_call(functools.partial(solve_body, own=own, planes=planes, bits...  5.09 us
    pallas_call x1, Pallas kernels, on_device(): pl.pallas_call(functools.partial(second_body, own=own, owner_bits=route.o...  4.7 us
    pallas_call x1, Pallas kernels, on_device(): pl.pallas_call(functools.partial(first_body, own=own, **sizes), out_shape...  4.12 us
    unnamed x21, local copies, waits for them, and re-layouts  3.67 us
    pallas_call x1, Pallas kernels, on_device(): pl.pallas_call(functools.partial(pack_body, own=own, planes=planes, strid...  1.45 us
  transfers between devices with their start and end apart: 14, of which 13 were waited for; matrix products, arithmetic and copies ran while one was open for 4% of the time, Pallas kernels for 7%

profile of v3, /device:TPU:0, one launch (start us, length us, event | category | flops | bytes accessed | tf_op | source)
XLA Modules:
  0.0 57.5 jit_solution(8701829725292059893)
XLA Ops:
  0.6 0.0 copy-start.7
  0.6 0.6 %copy-done.7 = bf16[2]{0:T(256)(128)(2,1)S(1)} copy-done((bf16[2]{0:T(256)(128)(2,1)S(1)}, bf16[2]{0:T(256)(128)(2,1)}, u32[]{:S(2)}) %copy-start.7) | copy-done | bytes 28
  1.3 0.6 %copy.9.occupation = bf16[2,1]{1,0:T(2,128)(2,1)} copy(bf16[2,1]{0,1:T(2,128)(2,1)S(1)} %bitcast.15) | data formatting | bytes 8 | tf_op jit(solution)/shard_map/reshape | solution.py:387
  1.9 1.5 %pack.1 = bf16[1,24,576]{2,1,0:T(8,128)(2,1)} custom-call(bf16[2,5760]{1,0:T(2,128)(2,1)} %orbitals.1, bf16[2,1]{1,0:T(2,128)(2,1)} %copy.9.occupation), custom_call_target="tpu_custom_call" | custom-call | tf_op jit(solution)/shard_map/pack/pallas_call | solution.py:381
  3.3 0.0 copy-start.3
  3.4 4.1 %collective-permute-start = (bf16[1,24,576]{2,1,0:T(8,128)(2,1)}, bf16[1,24,576]{2,1,0:T(8,128)(2,1)S(1)}, u32[]{:S(2)}, u32[]{:S(2)}) collective-permute-start(bf16[1,24,576]{2,1,0:T(8,128)(2,1)} %pack.1), channel_id=1, source_target_pairs={{0,16},{1,17},{2,18},{3,19},{4,20},{5,21},{6,22},{7,23},{8,24},{9,... | collective-permute-start | bytes 82952 | tf_op jit(solution)/shard_map/ppermute | solution.py:127
  7.4 0.8 %constant_dynamic-update-slice_fusion.5 = bf16[16,24,576]{2,1,0:T(8,128)(2,1)S(1)} fusion(bf16[1,24,576]{2,1,0:T(8,128)(2,1)} %pack.1), kind=kLoop, calls=%fused_computation.12 | loop fusion | bytes 58368
  8.2 1.7 %collective-permute-done = bf16[1,24,576]{2,1,0:T(8,128)(2,1)S(1)} collective-permute-done((bf16[1,24,576]{2,1,0:T(8,128)(2,1)}, bf16[1,24,576]{2,1,0:T(8,128)(2,1)S(1)}, u32[]{:S(2)}, u32[]{:S(2)}) %collective-permute-start) | collective-permute-done | bytes 27680 | tf_op jit(solution)/shard_map/ppermute | solution.py:127
  9.9 0.0 copy-done.3
  9.9 1.6 %collective-permute-start.1 = (bf16[2,24,576]{2,1,0:T(8,128)(2,1)S(1)}, bf16[2,24,576]{2,1,0:T(8,128)(2,1)S(1)}, u32[]{:S(2)}, u32[]{:S(2)}) collective-permute-start(bf16[2,24,576]{2,1,0:T(8,128)(2,1)S(1)} %pad_maximum_fusion.3), channel_id=1, source_target_pairs={{0,8},{1,9},{2,10},{3,11},{4,12},{5,13},{6,14},{7,15},{8,0},{9,1},... | collective-permute-start | bytes 165896 | tf_op jit(solution)/shard_map/ppermute | solution.py:127
  11.5 2.7 %collective-permute-done.1 = bf16[2,24,576]{2,1,0:T(8,128)(2,1)S(1)} collective-permute-done((bf16[2,24,576]{2,1,0:T(8,128)(2,1)S(1)}, bf16[2,24,576]{2,1,0:T(8,128)(2,1)S(1)}, u32[]{:S(2)}, u32[]{:S(2)}) %collective-permute-start.1) | collective-permute-done | bytes 55328 | tf_op jit(solution)/shard_map/ppermute | solution.py:127
  14.2 1.7 %collective-permute-start.2 = (bf16[4,24,576]{2,1,0:T(8,128)(2,1)S(1)}, bf16[4,24,576]{2,1,0:T(8,128)(2,1)S(1)}, u32[]{:S(2)}, u32[]{:S(2)}) collective-permute-start(bf16[4,24,576]{2,1,0:T(8,128)(2,1)S(1)} %pad_maximum_fusion.2), channel_id=1, source_target_pairs={{0,1},{1,0},{2,3},{3,2},{4,5},{5,4},{6,7},{7,6},{8,9},{9,8},{10,11... | collective-permute-start | bytes 331784 | tf_op jit(solution)/shard_map/ppermute | solution.py:127
  15.9 1.5 %collective-permute-start.3 = (bf16[4,24,576]{2,1,0:T(8,128)(2,1)S(1)}, bf16[4,24,576]{2,1,0:T(8,128)(2,1)S(1)}, u32[]{:S(2)}, u32[]{:S(2)}) collective-permute-start(bf16[4,24,576]{2,1,0:T(8,128)(2,1)S(1)} %pad_maximum_fusion.2), channel_id=1, source_target_pairs={{0,4},{1,5},{2,6},{3,7},{4,0},{5,1},{6,2},{7,3},{8,12},{9,13},{10,... | collective-permute-start | bytes 331784 | tf_op jit(solution)/shard_map/ppermute | solution.py:127
  17.5 0.3 collective-permute-start.4
  17.8 1.7 %collective-permute-done.2 = bf16[4,24,576]{2,1,0:T(8,128)(2,1)S(1)} collective-permute-done((bf16[4,24,576]{2,1,0:T(8,128)(2,1)S(1)}, bf16[4,24,576]{2,1,0:T(8,128)(2,1)S(1)}, u32[]{:S(2)}, u32[]{:S(2)}) %collective-permute-start.2) | collective-permute-done | bytes 110624 | tf_op jit(solution)/shard_map/ppermute | solution.py:127
  19.5 1.4 %collective-permute-done.3 = bf16[4,24,576]{2,1,0:T(8,128)(2,1)S(1)} collective-permute-done((bf16[4,24,576]{2,1,0:T(8,128)(2,1)S(1)}, bf16[4,24,576]{2,1,0:T(8,128)(2,1)S(1)}, u32[]{:S(2)}, u32[]{:S(2)}) %collective-permute-start.3) | collective-permute-done | bytes 110624 | tf_op jit(solution)/shard_map/ppermute | solution.py:127
  20.8 2.4 %collective-permute-done.4 = bf16[4,24,576]{2,1,0:T(8,128)(2,1)S(1)} collective-permute-done((bf16[4,24,576]{2,1,0:T(8,128)(2,1)S(1)}, bf16[4,24,576]{2,1,0:T(8,128)(2,1)S(1)}, u32[]{:S(2)}, u32[]{:S(2)}) %collective-permute-start.4) | collective-permute-done | bytes 110624 | tf_op jit(solution)/shard_map/ppermute | solution.py:127
  23.3 0.0 copy-start
  23.3 0.1 collective-permute-start.5
  23.4 0.7 %pad_add_fusion.place = s32[3]{0:T(128)} fusion(s32[1]{0:T(128)} %bitcast.2, s32[1]{0:T(128)} %bitcast.1, s32[1]{0:T(128)} %bitcast), kind=kLoop, calls=%fused_computation.13 | loop fusion | flops 6 | bytes 24 | tf_op jit(solution)/shard_map/stack | solution.py:375
  24.0 0.0 copy-done
  24.1 4.1 %near_pairs.1.before = f32[2,24,576]{2,1,0:T(8,128)} custom-call(s32[3]{0:T(128)} %pad_add_fusion.place, bf16[16,24,576]{2,1,0:T(8,128)(2,1)} %copy-done, bf16[2,192,192]{2,1,0:T(8,128)(2,1)} %constant.20.clone.mix_x, bf16[576,640]{1,0:T(8,128)(2,1)} %constant.21.clone.mix_y, bf16[256,256]{1,0:T(8,128)(2,1)} %constant.22.clone.mix_z, ...), custom_call_target="tpu_custom_call" | custom-call | tf_op jit(solution)/shard_map/near_pairs/pallas_call | solution.py:397
  28.2 0.0 collective-permute-done.5.other
  28.2 0.0 copy-start.2
  28.2 0.8 %copy-done.2 = bf16[16,24,576]{2,1,0:T(8,128)(2,1)} copy-done((bf16[16,24,576]{2,1,0:T(8,128)(2,1)}, bf16[16,24,576]{2,1,0:T(8,128)(2,1)S(1)}, u32[]{:S(2)}) %copy-start.2) | copy-done | bytes 442392
  29.0 4.7 %far_pairs.1 = (bf16[2,16,576]{2,1,0:T(8,128)(2,1)}, f32[2,16,576]{2,1,0:T(8,128)}) custom-call(s32[3]{0:T(128)} %pad_add_fusion.place, bf16[16,24,576]{2,1,0:T(8,128)(2,1)} %copy-done, bf16[16,24,576]{2,1,0:T(8,128)(2,1)} %copy-done.2, bf16[2,192,192]{2,1,0:T(8,128)(2,1)} %constant.20.clone.mix_x, bf16[576,640]{1,0:T(8,128)(2,1)} %constant.21.clone.mix_y, ...), custom_call_target="tpu_custom_call" | custom-call | tf_op jit(solution)/shard_map/far_pairs/pallas_call | solution.py:405
  33.7 3.6 %collective-permute-start.8 = (bf16[2,1,16,576]{3,2,1,0:T(8,128)(2,1)}, bf16[2,1,16,576]{3,2,1,0:T(8,128)(2,1)S(1)}, u32[]{:S(2)}, u32[]{:S(2)}) collective-permute-start(bf16[2,1,16,576]{3,2,1,0:T(8,128)(2,1)} %bitcast.11), channel_id=1, source_target_pairs={{0,24},{1,25},{2,26},{3,27},{4,28},{5,29},{6,30},{7,31},{8,16},{9,... | collective-permute-start | bytes 110600 | tf_op jit(solution)/shard_map/ppermute | solution.py:127
  37.3 0.0 collective-permute-start.7
  37.3 0.8 %collective-permute-start.6 = (bf16[2,1,16,576]{3,2,1,0:T(8,128)(2,1)}, bf16[2,1,16,576]{3,2,1,0:T(8,128)(2,1)S(1)}, u32[]{:S(2)}, u32[]{:S(2)}) collective-permute-start(bf16[2,1,16,576]{3,2,1,0:T(8,128)(2,1)} %bitcast.13), channel_id=1, source_target_pairs={{0,16},{1,17},{2,18},{3,19},{4,20},{5,21},{6,22},{7,23},{8,24},{9,... | collective-permute-start | bytes 110600 | tf_op jit(solution)/shard_map/ppermute | solution.py:127
  38.1 0.0 copy-start.5
  38.1 0.8 %slice_bitcast_fusion.2 = f32[16,576]{1,0:T(8,128)S(1)} fusion(f32[2,16,576]{2,1,0:T(8,128)} %get-tuple-element.7.kept), kind=kLoop, calls=%fused_computation.6 | loop fusion | bytes 73728 | tf_op jit(solution)/shard_map/squeeze | solution.py:418
  38.9 0.5 collective-permute-start.9
  39.4 0.7 %collective-permute-done.8 = bf16[2,1,16,576]{3,2,1,0:T(8,128)(2,1)S(1)} collective-permute-done((bf16[2,1,16,576]{3,2,1,0:T(8,128)(2,1)}, bf16[2,1,16,576]{3,2,1,0:T(8,128)(2,1)S(1)}, u32[]{:S(2)}, u32[]{:S(2)}) %collective-permute-start.8) | collective-permute-done | bytes 36896 | tf_op jit(solution)/shard_map/ppermute | solution.py:127
  40.1 1.8 %collective-permute-done.7 = bf16[2,1,16,576]{3,2,1,0:T(8,128)(2,1)S(1)} collective-permute-done((bf16[2,1,16,576]{3,2,1,0:T(8,128)(2,1)}, bf16[2,1,16,576]{3,2,1,0:T(8,128)(2,1)S(1)}, u32[]{:S(2)}, u32[]{:S(2)}) %collective-permute-start.7) | collective-permute-done | bytes 36896 | tf_op jit(solution)/shard_map/ppermute | solution.py:127
  41.9 0.5 collective-permute-done.6
  42.4 0.0 copy-done.5
  42.4 0.4 collective-permute-done.9.partner
  42.9 0.0 copy-start.6
  42.9 0.6 %copy-done.6 = f32[16,576]{1,0:T(8,128)} copy-done((f32[16,576]{1,0:T(8,128)}, f32[16,576]{1,0:T(8,128)S(1)}, u32[]{:S(2)}) %copy-start.6) | copy-done | bytes 36888
  43.5 0.4 collective-permute-start.12
  43.9 1.6 %collective-permute-start.11 = (bf16[4,16,576]{2,1,0:T(8,128)(2,1)S(1)}, bf16[4,16,576]{2,1,0:T(8,128)(2,1)S(1)}, u32[]{:S(2)}, u32[]{:S(2)}) collective-permute-start(bf16[4,16,576]{2,1,0:T(8,128)(2,1)S(1)} %get-tuple-element.10), channel_id=1, source_target_pairs={{0,4},{1,5},{2,6},{3,7},{4,0},{5,1},{6,2},{7,3},{8,12},{9,13},{10,... | collective-permute-start | bytes 221192 | tf_op jit(solution)/shard_map/ppermute | solution.py:127
  45.5 1.5 %collective-permute-start.10 = (bf16[4,16,576]{2,1,0:T(8,128)(2,1)S(1)}, bf16[4,16,576]{2,1,0:T(8,128)(2,1)S(1)}, u32[]{:S(2)}, u32[]{:S(2)}) collective-permute-start(bf16[4,16,576]{2,1,0:T(8,128)(2,1)S(1)} %get-tuple-element.11), channel_id=1, source_target_pairs={{0,1},{1,0},{2,3},{3,2},{4,5},{5,4},{6,7},{7,6},{8,9},{9,8},{10,11... | collective-permute-start | bytes 221192 | tf_op jit(solution)/shard_map/ppermute | solution.py:127
  47.0 1.9 %collective-permute-done.12 = bf16[4,16,576]{2,1,0:T(8,128)(2,1)S(1)} collective-permute-done((bf16[4,16,576]{2,1,0:T(8,128)(2,1)S(1)}, bf16[4,16,576]{2,1,0:T(8,128)(2,1)S(1)}, u32[]{:S(2)}, u32[]{:S(2)}) %collective-permute-start.12) | collective-permute-done | bytes 73760 | tf_op jit(solution)/shard_map/ppermute | solution.py:127
  48.9 0.3 collective-permute-done.11
  49.2 0.7 %collective-permute-done.10 = bf16[4,16,576]{2,1,0:T(8,128)(2,1)S(1)} collective-permute-done((bf16[4,16,576]{2,1,0:T(8,128)(2,1)S(1)}, bf16[4,16,576]{2,1,0:T(8,128)(2,1)S(1)}, u32[]{:S(2)}, u32[]{:S(2)}) %collective-permute-start.10) | collective-permute-done | bytes 73760 | tf_op jit(solution)/shard_map/ppermute | solution.py:127
  49.9 0.1 pad_maximum_fusion.local
  50.0 0.0 copy-start.1
  50.0 0.1 collective-permute-start.13
  50.1 1.6 %collective-permute-done.13.other = bf16[16,16,576]{2,1,0:T(8,128)(2,1)S(1)} collective-permute-done((bf16[16,16,576]{2,1,0:T(8,128)(2,1)S(1)}, bf16[16,16,576]{2,1,0:T(8,128)(2,1)S(1)}, u32[]{:S(2)}, u32[]{:S(2)}) %collective-permute-start.13) | collective-permute-done | bytes 294944 | tf_op jit(solution)/shard_map/ppermute | solution.py:127
  51.7 0.0 copy-done.1
  51.7 0.0 copy-start.4
  51.7 0.7 %copy-done.4 = bf16[16,16,576]{2,1,0:T(8,128)(2,1)} copy-done((bf16[16,16,576]{2,1,0:T(8,128)(2,1)}, bf16[16,16,576]{2,1,0:T(8,128)(2,1)S(1)}, u32[]{:S(2)}) %copy-start.4) | copy-done | bytes 294936
  52.4 5.1 %solve.1 = (f32[2,5760]{1,0:T(2,128)}, f32[2,5760]{1,0:T(2,128)}) custom-call(s32[3]{0:T(128)} %pad_add_fusion.place, bf16[16,16,576]{2,1,0:T(8,128)(2,1)} %copy-done.1, bf16[16,16,576]{2,1,0:T(8,128)(2,1)} %copy-done.4, f32[2,16,576]{2,1,0:T(8,128)} %get-tuple-element.7.kept, f32[16,576]{1,0:T(8,128)} %copy-done.6), custom_call_target="tpu_custom_call" | custom-call | tf_op jit(solution)/shard_map/solve/pallas_call | solution.py:433
  (9 shorter events, 0.2 us)
Async XLA Ops:
  0.6 0.7 %copy-start.7 = (bf16[2]{0:T(256)(128)(2,1)S(1)}, bf16[2]{0:T(256)(128)(2,1)}, u32[]{:S(2)}) copy-start(bf16[2]{0:T(256)(128)(2,1)} %param.8) | copy-start | bytes 16
  3.3 6.5 %copy-start.3 = (bf16[1,24,576]{2,1,0:T(8,128)(2,1)S(1)}, bf16[1,24,576]{2,1,0:T(8,128)(2,1)}, u32[]{:S(2)}) copy-start(bf16[1,24,576]{2,1,0:T(8,128)(2,1)} %pack.1) | copy-start | bytes 82948
  3.4 6.5 %collective-permute-start = (bf16[1,24,576]{2,1,0:T(8,128)(2,1)}, bf16[1,24,576]{2,1,0:T(8,128)(2,1)S(1)}, u32[]{:S(2)}, u32[]{:S(2)}) collective-permute-start(bf16[1,24,576]{2,1,0:T(8,128)(2,1)} %pack.1), channel_id=1, source_target_pairs={{0,16},{1,17},{2,18},{3,19},{4,20},{5,21},{6,22},{7,23},{8,24},{9,... | collective-permute-start | bytes 82952 | tf_op jit(solution)/shard_map/ppermute | solution.py:127
  9.9 4.3 %collective-permute-start.1 = (bf16[2,24,576]{2,1,0:T(8,128)(2,1)S(1)}, bf16[2,24,576]{2,1,0:T(8,128)(2,1)S(1)}, u32[]{:S(2)}, u32[]{:S(2)}) collective-permute-start(bf16[2,24,576]{2,1,0:T(8,128)(2,1)S(1)} %pad_maximum_fusion.3), channel_id=1, source_target_pairs={{0,8},{1,9},{2,10},{3,11},{4,12},{5,13},{6,14},{7,15},{8,0},{9,1},... | collective-permute-start | bytes 165896 | tf_op jit(solution)/shard_map/ppermute | solution.py:127
  14.2 5.2 %collective-permute-start.2 = (bf16[4,24,576]{2,1,0:T(8,128)(2,1)S(1)}, bf16[4,24,576]{2,1,0:T(8,128)(2,1)S(1)}, u32[]{:S(2)}, u32[]{:S(2)}) collective-permute-start(bf16[4,24,576]{2,1,0:T(8,128)(2,1)S(1)} %pad_maximum_fusion.2), channel_id=1, source_target_pairs={{0,1},{1,0},{2,3},{3,2},{4,5},{5,4},{6,7},{7,6},{8,9},{9,8},{10,11... | collective-permute-start | bytes 331784 | tf_op jit(solution)/shard_map/ppermute | solution.py:127
  15.9 4.9 %collective-permute-start.3 = (bf16[4,24,576]{2,1,0:T(8,128)(2,1)S(1)}, bf16[4,24,576]{2,1,0:T(8,128)(2,1)S(1)}, u32[]{:S(2)}, u32[]{:S(2)}) collective-permute-start(bf16[4,24,576]{2,1,0:T(8,128)(2,1)S(1)} %pad_maximum_fusion.2), channel_id=1, source_target_pairs={{0,4},{1,5},{2,6},{3,7},{4,0},{5,1},{6,2},{7,3},{8,12},{9,13},{10,... | collective-permute-start | bytes 331784 | tf_op jit(solution)/shard_map/ppermute | solution.py:127
  17.5 5.8 %collective-permute-start.4 = (bf16[4,24,576]{2,1,0:T(8,128)(2,1)S(1)}, bf16[4,24,576]{2,1,0:T(8,128)(2,1)S(1)}, u32[]{:S(2)}, u32[]{:S(2)}) collective-permute-start(bf16[4,24,576]{2,1,0:T(8,128)(2,1)S(1)} %pad_maximum_fusion.2), channel_id=1, source_target_pairs={{0,5},{1,4},{2,7},{3,6},{4,1},{5,0},{6,3},{7,2},{8,13},{9,12},{10,... | collective-permute-start | bytes 331784 | tf_op jit(solution)/shard_map/ppermute | solution.py:127
  23.3 0.8 %copy-start = (bf16[16,24,576]{2,1,0:T(8,128)(2,1)}, bf16[16,24,576]{2,1,0:T(8,128)(2,1)S(1)}, u32[]{:S(2)}) copy-start(bf16[16,24,576]{2,1,0:T(8,128)(2,1)S(1)} %constant_dynamic-update-slice_fusion.local) | copy-start | bytes 1327108
  23.3 4.9 %collective-permute-start.5 = (bf16[16,24,576]{2,1,0:T(8,128)(2,1)S(1)}, bf16[16,24,576]{2,1,0:T(8,128)(2,1)S(1)}, u32[]{:S(2)}, u32[]{:S(2)}) collective-permute-start(bf16[16,24,576]{2,1,0:T(8,128)(2,1)S(1)} %constant_dynamic-update-slice_fusion.local), channel_id=1, source_target_pairs={{0,2},{1,3},{2,0},{3,1},{4,6},{5,7},{6,4},{7,5},{8,10},{9,11},{10,... | collective-permute-start | bytes 1327112 | tf_op jit(solution)/shard_map/ppermute | solution.py:127
  28.2 0.8 %copy-start.2 = (bf16[16,24,576]{2,1,0:T(8,128)(2,1)}, bf16[16,24,576]{2,1,0:T(8,128)(2,1)S(1)}, u32[]{:S(2)}) copy-start(bf16[16,24,576]{2,1,0:T(8,128)(2,1)S(1)} %collective-permute-done.5.other) | copy-start | bytes 1327108
  33.7 6.4 %collective-permute-start.8 = (bf16[2,1,16,576]{3,2,1,0:T(8,128)(2,1)}, bf16[2,1,16,576]{3,2,1,0:T(8,128)(2,1)S(1)}, u32[]{:S(2)}, u32[]{:S(2)}) collective-permute-start(bf16[2,1,16,576]{3,2,1,0:T(8,128)(2,1)} %bitcast.11), channel_id=1, source_target_pairs={{0,24},{1,25},{2,26},{3,27},{4,28},{5,29},{6,30},{7,31},{8,16},{9,... | collective-permute-start | bytes 110600 | tf_op jit(solution)/shard_map/ppermute | solution.py:127
  37.3 4.7 %collective-permute-start.7 = (bf16[2,1,16,576]{3,2,1,0:T(8,128)(2,1)}, bf16[2,1,16,576]{3,2,1,0:T(8,128)(2,1)S(1)}, u32[]{:S(2)}, u32[]{:S(2)}) collective-permute-start(bf16[2,1,16,576]{3,2,1,0:T(8,128)(2,1)} %bitcast.12), channel_id=1, source_target_pairs={{0,8},{1,9},{2,10},{3,11},{4,12},{5,13},{6,14},{7,15},{8,0},{9,1},... | collective-permute-start | bytes 110600 | tf_op jit(solution)/shard_map/ppermute | solution.py:127
  37.3 5.1 %collective-permute-start.6 = (bf16[2,1,16,576]{3,2,1,0:T(8,128)(2,1)}, bf16[2,1,16,576]{3,2,1,0:T(8,128)(2,1)S(1)}, u32[]{:S(2)}, u32[]{:S(2)}) collective-permute-start(bf16[2,1,16,576]{3,2,1,0:T(8,128)(2,1)} %bitcast.13), channel_id=1, source_target_pairs={{0,16},{1,17},{2,18},{3,19},{4,20},{5,21},{6,22},{7,23},{8,24},{9,... | collective-permute-start | bytes 110600 | tf_op jit(solution)/shard_map/ppermute | solution.py:127
  38.1 4.3 %copy-start.5 = (bf16[2,16,576]{2,1,0:T(8,128)(2,1)S(1)}, bf16[2,16,576]{2,1,0:T(8,128)(2,1)}, u32[]{:S(2)}) copy-start(bf16[2,16,576]{2,1,0:T(8,128)(2,1)} %get-tuple-element.6) | copy-start | bytes 110596
  38.9 4.0 %collective-permute-start.9 = (f32[16,576]{1,0:T(8,128)S(1)}, f32[16,576]{1,0:T(8,128)S(1)}, u32[]{:S(2)}, u32[]{:S(2)}) collective-permute-start(f32[16,576]{1,0:T(8,128)S(1)} %slice_bitcast_fusion.2), channel_id=1, source_target_pairs={{0,1},{1,0},{2,3},{3,2},{4,5},{5,4},{6,7},{7,6},{8,9},{9,8},{10,11... | collective-permute-start | bytes 110600 | tf_op jit(solution)/shard_map/ppermute | solution.py:127
  42.9 0.6 %copy-start.6 = (f32[16,576]{1,0:T(8,128)}, f32[16,576]{1,0:T(8,128)S(1)}, u32[]{:S(2)}) copy-start(f32[16,576]{1,0:T(8,128)S(1)} %collective-permute-done.9.partner) | copy-start | bytes 110596
  43.5 5.4 %collective-permute-start.12 = (bf16[4,16,576]{2,1,0:T(8,128)(2,1)S(1)}, bf16[4,16,576]{2,1,0:T(8,128)(2,1)S(1)}, u32[]{:S(2)}, u32[]{:S(2)}) collective-permute-start(bf16[4,16,576]{2,1,0:T(8,128)(2,1)S(1)} %get-tuple-element.11), channel_id=1, source_target_pairs={{0,5},{1,4},{2,7},{3,6},{4,1},{5,0},{6,3},{7,2},{8,13},{9,12},{10,... | collective-permute-start | bytes 221192 | tf_op jit(solution)/shard_map/ppermute | solution.py:127
  43.9 5.3 %collective-permute-start.11 = (bf16[4,16,576]{2,1,0:T(8,128)(2,1)S(1)}, bf16[4,16,576]{2,1,0:T(8,128)(2,1)S(1)}, u32[]{:S(2)}, u32[]{:S(2)}) collective-permute-start(bf16[4,16,576]{2,1,0:T(8,128)(2,1)S(1)} %get-tuple-element.10), channel_id=1, source_target_pairs={{0,4},{1,5},{2,6},{3,7},{4,0},{5,1},{6,2},{7,3},{8,12},{9,13},{10,... | collective-permute-start | bytes 221192 | tf_op jit(solution)/shard_map/ppermute | solution.py:127
  45.5 4.4 %collective-permute-start.10 = (bf16[4,16,576]{2,1,0:T(8,128)(2,1)S(1)}, bf16[4,16,576]{2,1,0:T(8,128)(2,1)S(1)}, u32[]{:S(2)}, u32[]{:S(2)}) collective-permute-start(bf16[4,16,576]{2,1,0:T(8,128)(2,1)S(1)} %get-tuple-element.11), channel_id=1, source_target_pairs={{0,1},{1,0},{2,3},{3,2},{4,5},{5,4},{6,7},{7,6},{8,9},{9,8},{10,11... | collective-permute-start | bytes 221192 | tf_op jit(solution)/shard_map/ppermute | solution.py:127
  50.0 1.7 %copy-start.1 = (bf16[16,16,576]{2,1,0:T(8,128)(2,1)}, bf16[16,16,576]{2,1,0:T(8,128)(2,1)S(1)}, u32[]{:S(2)}) copy-start(bf16[16,16,576]{2,1,0:T(8,128)(2,1)S(1)} %pad_maximum_fusion.local) | copy-start | bytes 884740
  50.0 1.7 %collective-permute-start.13 = (bf16[16,16,576]{2,1,0:T(8,128)(2,1)S(1)}, bf16[16,16,576]{2,1,0:T(8,128)(2,1)S(1)}, u32[]{:S(2)}, u32[]{:S(2)}) collective-permute-start(bf16[16,16,576]{2,1,0:T(8,128)(2,1)S(1)} %pad_maximum_fusion.local), channel_id=1, source_target_pairs={{0,2},{1,3},{2,0},{3,1},{4,6},{5,7},{6,4},{7,5},{8,10},{9,11},{10,... | collective-permute-start | bytes 884744 | tf_op jit(solution)/shard_map/ppermute | solution.py:127
  51.7 0.7 %copy-start.4 = (bf16[16,16,576]{2,1,0:T(8,128)(2,1)}, bf16[16,16,576]{2,1,0:T(8,128)(2,1)S(1)}, u32[]{:S(2)}) copy-start(bf16[16,16,576]{2,1,0:T(8,128)(2,1)S(1)} %collective-permute-done.13.other) | copy-start | bytes 884740

commit v4 on v3

--- a/solution.py
+++ b/solution.py
@@ -139,7 +139,7 @@
         for x in range(planes):
             lines.append(values[orbital : orbital + 1, x * PLANE : (x + 1) * PLANE])
         lines.append(
-            jnp.broadcast_to(weights[orbital : orbital + 1], (stride - planes, PLANE))
+            jnp.broadcast_to(weights[:, orbital : orbital + 1], (stride - planes, PLANE))
         )
     block[0] = jnp.concatenate(lines, axis=0).astype(BF16)
 
@@ -292,9 +292,11 @@
     column = lax.broadcasted_iota(jnp.int32, (norb, norb), 1)
     right = jnp.where(row == column, 1.0, 0.0).astype(F32)
     if norb <= 32:
+        both = jnp.concatenate([left, right], axis=1)
         for k in range(norb):
-            factor = jnp.where(row[:, :1] > k, left[:, k : k + 1] / left[k : k + 1, k : k + 1], 0.0)
-            left, right = left - factor * left[k : k + 1], right - factor * right[k : k + 1]
+            scaled = both[k : k + 1] / both[k : k + 1, k : k + 1]
+            both = both - jnp.where(row[:, :1] > k, both[:, k : k + 1], 0.0) * scaled
+        left, right = both[:, :norb], both[:, norb:]
     else:
         work[0] = left
         work[1] = right
@@ -384,7 +386,7 @@
         in_specs=[vmem, vmem],
         out_specs=vmem,
         name="pack",
-    )(orbitals, occupation.reshape(own, 1))
+    )(orbitals, occupation.reshape(1, own))
     for bit in reversed(route.rounds[0]):
         local = jnp.concatenate([local, route.swap(local, 1 << bit)])
     for members in route.rounds[1:-1]:

time: 57.9 us -> 56.8 us (0.981)
  local copies, waits for them, and re-layouts: 5.1 us -> 3.88 us
    reshape x1 -> x0, local copies, waits for them, and re-layouts: 0.61 us -> none  [on_device(): occupation.reshape(own, 1)]
    unnamed x21 -> x19, local copies, waits for them, and re-layouts: 3.67 us -> 3.06 us
where the time goes in v4:
time: 56.8 us; the launch traced here: 56.4 us
  waiting for transfers between devices  17.8 us (31%)
  starting transfers between devices  17.7 us (31%)
  Pallas kernels  15.5 us (27%)
  local copies, waits for them, and re-layouts  3.88 us (7%)
  other arithmetic  0.75 us (1%)
  between operations  0.71 us (1%)
    ppermute x14, waiting for transfers between devices, swap(): return lax.ppermute(array, ('orb', 'grid'), pairs)  17.8 us
    ppermute x14, starting transfers between devices, swap(): return lax.ppermute(array, ('orb', 'grid'), pairs)  17.7 us
    pallas_call x1, Pallas kernels, on_device(): pl.pallas_call(functools.partial(solve_body, own=own, planes=planes, bits...  5.21 us
    pallas_call x1, Pallas kernels, on_device(): pl.pallas_call(functools.partial(second_body, own=own, owner_bits=route.o...  4.7 us
    pallas_call x1, Pallas kernels, on_device(): pl.pallas_call(functools.partial(first_body, own=own, **sizes), out_shape...  4.14 us
    unnamed x19, local copies, waits for them, and re-layouts  3.06 us
    pallas_call x1, Pallas kernels, on_device(): pl.pallas_call(functools.partial(pack_body, own=own, planes=planes, strid...  1.45 us
  transfers between devices with their start and end apart: 14, of which 13 were waited for; matrix products, arithmetic and copies ran while one was open for 4% of the time, Pallas kernels for 7%

profile of v4, /device:TPU:0, one launch (start us, length us, event | category | flops | bytes accessed | tf_op | source)
XLA Modules:
  0.0 56.4 jit_solution(9532740011118820842)
XLA Ops:
  0.6 1.5 %pack.1 = bf16[1,24,576]{2,1,0:T(8,128)(2,1)} custom-call(bf16[2,5760]{1,0:T(2,128)(2,1)} %orbitals.1, bf16[1,2]{1,0:T(2,128)(2,1)} %bitcast.15), custom_call_target="tpu_custom_call" | custom-call | tf_op jit(solution)/shard_map/pack/pallas_call | solution.py:383
  2.1 0.0 copy-start.3
  2.1 4.1 %collective-permute-start = (bf16[1,24,576]{2,1,0:T(8,128)(2,1)}, bf16[1,24,576]{2,1,0:T(8,128)(2,1)S(1)}, u32[]{:S(2)}, u32[]{:S(2)}) collective-permute-start(bf16[1,24,576]{2,1,0:T(8,128)(2,1)} %pack.1), channel_id=1, source_target_pairs={{0,16},{1,17},{2,18},{3,19},{4,20},{5,21},{6,22},{7,23},{8,24},{9,... | collective-permute-start | bytes 82952 | tf_op jit(solution)/shard_map/ppermute | solution.py:127
  6.2 0.8 %constant_dynamic-update-slice_fusion.5 = bf16[16,24,576]{2,1,0:T(8,128)(2,1)S(1)} fusion(bf16[1,24,576]{2,1,0:T(8,128)(2,1)} %pack.1), kind=kLoop, calls=%fused_computation.12 | loop fusion | bytes 58368
  6.9 1.7 %collective-permute-done = bf16[1,24,576]{2,1,0:T(8,128)(2,1)S(1)} collective-permute-done((bf16[1,24,576]{2,1,0:T(8,128)(2,1)}, bf16[1,24,576]{2,1,0:T(8,128)(2,1)S(1)}, u32[]{:S(2)}, u32[]{:S(2)}) %collective-permute-start) | collective-permute-done | bytes 27680 | tf_op jit(solution)/shard_map/ppermute | solution.py:127
  8.6 0.0 copy-done.3
  8.7 1.6 %collective-permute-start.1 = (bf16[2,24,576]{2,1,0:T(8,128)(2,1)S(1)}, bf16[2,24,576]{2,1,0:T(8,128)(2,1)S(1)}, u32[]{:S(2)}, u32[]{:S(2)}) collective-permute-start(bf16[2,24,576]{2,1,0:T(8,128)(2,1)S(1)} %pad_maximum_fusion.3), channel_id=1, source_target_pairs={{0,8},{1,9},{2,10},{3,11},{4,12},{5,13},{6,14},{7,15},{8,0},{9,1},... | collective-permute-start | bytes 165896 | tf_op jit(solution)/shard_map/ppermute | solution.py:127
  10.2 2.7 %collective-permute-done.1 = bf16[2,24,576]{2,1,0:T(8,128)(2,1)S(1)} collective-permute-done((bf16[2,24,576]{2,1,0:T(8,128)(2,1)S(1)}, bf16[2,24,576]{2,1,0:T(8,128)(2,1)S(1)}, u32[]{:S(2)}, u32[]{:S(2)}) %collective-permute-start.1) | collective-permute-done | bytes 55328 | tf_op jit(solution)/shard_map/ppermute | solution.py:127
  13.0 1.7 %collective-permute-start.2 = (bf16[4,24,576]{2,1,0:T(8,128)(2,1)S(1)}, bf16[4,24,576]{2,1,0:T(8,128)(2,1)S(1)}, u32[]{:S(2)}, u32[]{:S(2)}) collective-permute-start(bf16[4,24,576]{2,1,0:T(8,128)(2,1)S(1)} %pad_maximum_fusion.2), channel_id=1, source_target_pairs={{0,1},{1,0},{2,3},{3,2},{4,5},{5,4},{6,7},{7,6},{8,9},{9,8},{10,11... | collective-permute-start | bytes 331784 | tf_op jit(solution)/shard_map/ppermute | solution.py:127
  14.7 1.5 %collective-permute-start.3 = (bf16[4,24,576]{2,1,0:T(8,128)(2,1)S(1)}, bf16[4,24,576]{2,1,0:T(8,128)(2,1)S(1)}, u32[]{:S(2)}, u32[]{:S(2)}) collective-permute-start(bf16[4,24,576]{2,1,0:T(8,128)(2,1)S(1)} %pad_maximum_fusion.2), channel_id=1, source_target_pairs={{0,4},{1,5},{2,6},{3,7},{4,0},{5,1},{6,2},{7,3},{8,12},{9,13},{10,... | collective-permute-start | bytes 331784 | tf_op jit(solution)/shard_map/ppermute | solution.py:127
  16.2 0.3 collective-permute-start.4
  16.5 1.7 %collective-permute-done.2 = bf16[4,24,576]{2,1,0:T(8,128)(2,1)S(1)} collective-permute-done((bf16[4,24,576]{2,1,0:T(8,128)(2,1)S(1)}, bf16[4,24,576]{2,1,0:T(8,128)(2,1)S(1)}, u32[]{:S(2)}, u32[]{:S(2)}) %collective-permute-start.2) | collective-permute-done | bytes 110624 | tf_op jit(solution)/shard_map/ppermute | solution.py:127
  18.2 1.4 %collective-permute-done.3 = bf16[4,24,576]{2,1,0:T(8,128)(2,1)S(1)} collective-permute-done((bf16[4,24,576]{2,1,0:T(8,128)(2,1)S(1)}, bf16[4,24,576]{2,1,0:T(8,128)(2,1)S(1)}, u32[]{:S(2)}, u32[]{:S(2)}) %collective-permute-start.3) | collective-permute-done | bytes 110624 | tf_op jit(solution)/shard_map/ppermute | solution.py:127
  19.6 2.4 %collective-permute-done.4 = bf16[4,24,576]{2,1,0:T(8,128)(2,1)S(1)} collective-permute-done((bf16[4,24,576]{2,1,0:T(8,128)(2,1)S(1)}, bf16[4,24,576]{2,1,0:T(8,128)(2,1)S(1)}, u32[]{:S(2)}, u32[]{:S(2)}) %collective-permute-start.4) | collective-permute-done | bytes 110624 | tf_op jit(solution)/shard_map/ppermute | solution.py:127
  22.0 0.0 copy-start
  22.0 0.1 collective-permute-start.5
  22.1 0.6 %pad_add_fusion.place = s32[3]{0:T(128)} fusion(s32[1]{0:T(128)} %bitcast.2, s32[1]{0:T(128)} %bitcast.1, s32[1]{0:T(128)} %bitcast), kind=kLoop, calls=%fused_computation.13 | loop fusion | flops 6 | bytes 24 | tf_op jit(solution)/shard_map/stack | solution.py:377
  22.7 0.1 copy-done
  22.8 4.1 %near_pairs.1.before = f32[2,24,576]{2,1,0:T(8,128)} custom-call(s32[3]{0:T(128)} %pad_add_fusion.place, bf16[16,24,576]{2,1,0:T(8,128)(2,1)} %copy-done, bf16[2,192,192]{2,1,0:T(8,128)(2,1)} %constant.20.clone.mix_x, bf16[576,640]{1,0:T(8,128)(2,1)} %constant.21.clone.mix_y, bf16[256,256]{1,0:T(8,128)(2,1)} %constant.22.clone.mix_z, ...), custom_call_target="tpu_custom_call" | custom-call | tf_op jit(solution)/shard_map/near_pairs/pallas_call | solution.py:399
  26.9 0.0 collective-permute-done.5.other
  26.9 0.0 copy-start.2
  26.9 0.8 %copy-done.2 = bf16[16,24,576]{2,1,0:T(8,128)(2,1)} copy-done((bf16[16,24,576]{2,1,0:T(8,128)(2,1)}, bf16[16,24,576]{2,1,0:T(8,128)(2,1)S(1)}, u32[]{:S(2)}) %copy-start.2) | copy-done | bytes 442392
  27.7 4.7 %far_pairs.1 = (bf16[2,16,576]{2,1,0:T(8,128)(2,1)}, f32[2,16,576]{2,1,0:T(8,128)}) custom-call(s32[3]{0:T(128)} %pad_add_fusion.place, bf16[16,24,576]{2,1,0:T(8,128)(2,1)} %copy-done, bf16[16,24,576]{2,1,0:T(8,128)(2,1)} %copy-done.2, bf16[2,192,192]{2,1,0:T(8,128)(2,1)} %constant.20.clone.mix_x, bf16[576,640]{1,0:T(8,128)(2,1)} %constant.21.clone.mix_y, ...), custom_call_target="tpu_custom_call" | custom-call | tf_op jit(solution)/shard_map/far_pairs/pallas_call | solution.py:407
  32.4 3.6 %collective-permute-start.8 = (bf16[2,1,16,576]{3,2,1,0:T(8,128)(2,1)}, bf16[2,1,16,576]{3,2,1,0:T(8,128)(2,1)S(1)}, u32[]{:S(2)}, u32[]{:S(2)}) collective-permute-start(bf16[2,1,16,576]{3,2,1,0:T(8,128)(2,1)} %bitcast.11), channel_id=1, source_target_pairs={{0,24},{1,25},{2,26},{3,27},{4,28},{5,29},{6,30},{7,31},{8,16},{9,... | collective-permute-start | bytes 110600 | tf_op jit(solution)/shard_map/ppermute | solution.py:127
  36.0 0.0 collective-permute-start.7
  36.0 0.8 %collective-permute-start.6 = (bf16[2,1,16,576]{3,2,1,0:T(8,128)(2,1)}, bf16[2,1,16,576]{3,2,1,0:T(8,128)(2,1)S(1)}, u32[]{:S(2)}, u32[]{:S(2)}) collective-permute-start(bf16[2,1,16,576]{3,2,1,0:T(8,128)(2,1)} %bitcast.13), channel_id=1, source_target_pairs={{0,16},{1,17},{2,18},{3,19},{4,20},{5,21},{6,22},{7,23},{8,24},{9,... | collective-permute-start | bytes 110600 | tf_op jit(solution)/shard_map/ppermute | solution.py:127
  36.8 0.0 copy-start.5
  36.8 0.8 %slice_bitcast_fusion.2 = f32[16,576]{1,0:T(8,128)S(1)} fusion(f32[2,16,576]{2,1,0:T(8,128)} %get-tuple-element.7.kept), kind=kLoop, calls=%fused_computation.6 | loop fusion | bytes 73728 | tf_op jit(solution)/shard_map/squeeze | solution.py:420
  37.6 0.5 collective-permute-start.9
  38.1 0.7 %collective-permute-done.8 = bf16[2,1,16,576]{3,2,1,0:T(8,128)(2,1)S(1)} collective-permute-done((bf16[2,1,16,576]{3,2,1,0:T(8,128)(2,1)}, bf16[2,1,16,576]{3,2,1,0:T(8,128)(2,1)S(1)}, u32[]{:S(2)}, u32[]{:S(2)}) %collective-permute-start.8) | collective-permute-done | bytes 36896 | tf_op jit(solution)/shard_map/ppermute | solution.py:127
  38.8 1.9 %collective-permute-done.7 = bf16[2,1,16,576]{3,2,1,0:T(8,128)(2,1)S(1)} collective-permute-done((bf16[2,1,16,576]{3,2,1,0:T(8,128)(2,1)}, bf16[2,1,16,576]{3,2,1,0:T(8,128)(2,1)S(1)}, u32[]{:S(2)}, u32[]{:S(2)}) %collective-permute-start.7) | collective-permute-done | bytes 36896 | tf_op jit(solution)/shard_map/ppermute | solution.py:127
  40.7 0.5 collective-permute-done.6
  41.1 0.0 copy-done.5
  41.2 0.4 collective-permute-done.9.partner
  41.6 0.0 copy-start.6
  41.6 0.6 %copy-done.6 = f32[16,576]{1,0:T(8,128)} copy-done((f32[16,576]{1,0:T(8,128)}, f32[16,576]{1,0:T(8,128)S(1)}, u32[]{:S(2)}) %copy-start.6) | copy-done | bytes 36888
  42.2 0.4 collective-permute-start.12
  42.6 1.6 %collective-permute-start.11 = (bf16[4,16,576]{2,1,0:T(8,128)(2,1)S(1)}, bf16[4,16,576]{2,1,0:T(8,128)(2,1)S(1)}, u32[]{:S(2)}, u32[]{:S(2)}) collective-permute-start(bf16[4,16,576]{2,1,0:T(8,128)(2,1)S(1)} %get-tuple-element.10), channel_id=1, source_target_pairs={{0,4},{1,5},{2,6},{3,7},{4,0},{5,1},{6,2},{7,3},{8,12},{9,13},{10,... | collective-permute-start | bytes 221192 | tf_op jit(solution)/shard_map/ppermute | solution.py:127
  44.2 1.5 %collective-permute-start.10 = (bf16[4,16,576]{2,1,0:T(8,128)(2,1)S(1)}, bf16[4,16,576]{2,1,0:T(8,128)(2,1)S(1)}, u32[]{:S(2)}, u32[]{:S(2)}) collective-permute-start(bf16[4,16,576]{2,1,0:T(8,128)(2,1)S(1)} %get-tuple-element.11), channel_id=1, source_target_pairs={{0,1},{1,0},{2,3},{3,2},{4,5},{5,4},{6,7},{7,6},{8,9},{9,8},{10,11... | collective-permute-start | bytes 221192 | tf_op jit(solution)/shard_map/ppermute | solution.py:127
  45.7 1.9 %collective-permute-done.12 = bf16[4,16,576]{2,1,0:T(8,128)(2,1)S(1)} collective-permute-done((bf16[4,16,576]{2,1,0:T(8,128)(2,1)S(1)}, bf16[4,16,576]{2,1,0:T(8,128)(2,1)S(1)}, u32[]{:S(2)}, u32[]{:S(2)}) %collective-permute-start.12) | collective-permute-done | bytes 73760 | tf_op jit(solution)/shard_map/ppermute | solution.py:127
  47.7 0.3 collective-permute-done.11
  47.9 0.7 %collective-permute-done.10 = bf16[4,16,576]{2,1,0:T(8,128)(2,1)S(1)} collective-permute-done((bf16[4,16,576]{2,1,0:T(8,128)(2,1)S(1)}, bf16[4,16,576]{2,1,0:T(8,128)(2,1)S(1)}, u32[]{:S(2)}, u32[]{:S(2)}) %collective-permute-start.10) | collective-permute-done | bytes 73760 | tf_op jit(solution)/shard_map/ppermute | solution.py:127
  48.7 0.1 pad_maximum_fusion.local
  48.7 0.0 copy-start.1
  48.7 0.1 collective-permute-start.13
  48.8 1.6 %collective-permute-done.13.other = bf16[16,16,576]{2,1,0:T(8,128)(2,1)S(1)} collective-permute-done((bf16[16,16,576]{2,1,0:T(8,128)(2,1)S(1)}, bf16[16,16,576]{2,1,0:T(8,128)(2,1)S(1)}, u32[]{:S(2)}, u32[]{:S(2)}) %collective-permute-start.13) | collective-permute-done | bytes 294944 | tf_op jit(solution)/shard_map/ppermute | solution.py:127
  50.4 0.0 copy-done.1
  50.4 0.0 copy-start.4
  50.4 0.7 %copy-done.4 = bf16[16,16,576]{2,1,0:T(8,128)(2,1)} copy-done((bf16[16,16,576]{2,1,0:T(8,128)(2,1)}, bf16[16,16,576]{2,1,0:T(8,128)(2,1)S(1)}, u32[]{:S(2)}) %copy-start.4) | copy-done | bytes 294936
  51.2 5.2 %solve.1 = (f32[2,5760]{1,0:T(2,128)}, f32[2,5760]{1,0:T(2,128)}) custom-call(s32[3]{0:T(128)} %pad_add_fusion.place, bf16[16,16,576]{2,1,0:T(8,128)(2,1)} %copy-done.1, bf16[16,16,576]{2,1,0:T(8,128)(2,1)} %copy-done.4, f32[2,16,576]{2,1,0:T(8,128)} %get-tuple-element.7.kept, f32[16,576]{1,0:T(8,128)} %copy-done.6), custom_call_target="tpu_custom_call" | custom-call | tf_op jit(solution)/shard_map/solve/pallas_call | solution.py:435
  (9 shorter events, 0.2 us)
Async XLA Ops:
  2.1 6.5 %copy-start.3 = (bf16[1,24,576]{2,1,0:T(8,128)(2,1)S(1)}, bf16[1,24,576]{2,1,0:T(8,128)(2,1)}, u32[]{:S(2)}) copy-start(bf16[1,24,576]{2,1,0:T(8,128)(2,1)} %pack.1) | copy-start | bytes 82948
  2.1 6.5 %collective-permute-start = (bf16[1,24,576]{2,1,0:T(8,128)(2,1)}, bf16[1,24,576]{2,1,0:T(8,128)(2,1)S(1)}, u32[]{:S(2)}, u32[]{:S(2)}) collective-permute-start(bf16[1,24,576]{2,1,0:T(8,128)(2,1)} %pack.1), channel_id=1, source_target_pairs={{0,16},{1,17},{2,18},{3,19},{4,20},{5,21},{6,22},{7,23},{8,24},{9,... | collective-permute-start | bytes 82952 | tf_op jit(solution)/shard_map/ppermute | solution.py:127
  8.7 4.3 %collective-permute-start.1 = (bf16[2,24,576]{2,1,0:T(8,128)(2,1)S(1)}, bf16[2,24,576]{2,1,0:T(8,128)(2,1)S(1)}, u32[]{:S(2)}, u32[]{:S(2)}) collective-permute-start(bf16[2,24,576]{2,1,0:T(8,128)(2,1)S(1)} %pad_maximum_fusion.3), channel_id=1, source_target_pairs={{0,8},{1,9},{2,10},{3,11},{4,12},{5,13},{6,14},{7,15},{8,0},{9,1},... | collective-permute-start | bytes 165896 | tf_op jit(solution)/shard_map/ppermute | solution.py:127
  13.0 5.2 %collective-permute-start.2 = (bf16[4,24,576]{2,1,0:T(8,128)(2,1)S(1)}, bf16[4,24,576]{2,1,0:T(8,128)(2,1)S(1)}, u32[]{:S(2)}, u32[]{:S(2)}) collective-permute-start(bf16[4,24,576]{2,1,0:T(8,128)(2,1)S(1)} %pad_maximum_fusion.2), channel_id=1, source_target_pairs={{0,1},{1,0},{2,3},{3,2},{4,5},{5,4},{6,7},{7,6},{8,9},{9,8},{10,11... | collective-permute-start | bytes 331784 | tf_op jit(solution)/shard_map/ppermute | solution.py:127
  14.7 4.9 %collective-permute-start.3 = (bf16[4,24,576]{2,1,0:T(8,128)(2,1)S(1)}, bf16[4,24,576]{2,1,0:T(8,128)(2,1)S(1)}, u32[]{:S(2)}, u32[]{:S(2)}) collective-permute-start(bf16[4,24,576]{2,1,0:T(8,128)(2,1)S(1)} %pad_maximum_fusion.2), channel_id=1, source_target_pairs={{0,4},{1,5},{2,6},{3,7},{4,0},{5,1},{6,2},{7,3},{8,12},{9,13},{10,... | collective-permute-start | bytes 331784 | tf_op jit(solution)/shard_map/ppermute | solution.py:127
  16.2 5.8 %collective-permute-start.4 = (bf16[4,24,576]{2,1,0:T(8,128)(2,1)S(1)}, bf16[4,24,576]{2,1,0:T(8,128)(2,1)S(1)}, u32[]{:S(2)}, u32[]{:S(2)}) collective-permute-start(bf16[4,24,576]{2,1,0:T(8,128)(2,1)S(1)} %pad_maximum_fusion.2), channel_id=1, source_target_pairs={{0,5},{1,4},{2,7},{3,6},{4,1},{5,0},{6,3},{7,2},{8,13},{9,12},{10,... | collective-permute-start | bytes 331784 | tf_op jit(solution)/shard_map/ppermute | solution.py:127
  22.0 0.8 %copy-start = (bf16[16,24,576]{2,1,0:T(8,128)(2,1)}, bf16[16,24,576]{2,1,0:T(8,128)(2,1)S(1)}, u32[]{:S(2)}) copy-start(bf16[16,24,576]{2,1,0:T(8,128)(2,1)S(1)} %constant_dynamic-update-slice_fusion.local) | copy-start | bytes 1327108
  22.0 4.9 %collective-permute-start.5 = (bf16[16,24,576]{2,1,0:T(8,128)(2,1)S(1)}, bf16[16,24,576]{2,1,0:T(8,128)(2,1)S(1)}, u32[]{:S(2)}, u32[]{:S(2)}) collective-permute-start(bf16[16,24,576]{2,1,0:T(8,128)(2,1)S(1)} %constant_dynamic-update-slice_fusion.local), channel_id=1, source_target_pairs={{0,2},{1,3},{2,0},{3,1},{4,6},{5,7},{6,4},{7,5},{8,10},{9,11},{10,... | collective-permute-start | bytes 1327112 | tf_op jit(solution)/shard_map/ppermute | solution.py:127
  26.9 0.8 %copy-start.2 = (bf16[16,24,576]{2,1,0:T(8,128)(2,1)}, bf16[16,24,576]{2,1,0:T(8,128)(2,1)S(1)}, u32[]{:S(2)}) copy-start(bf16[16,24,576]{2,1,0:T(8,128)(2,1)S(1)} %collective-permute-done.5.other) | copy-start | bytes 1327108
  32.4 6.4 %collective-permute-start.8 = (bf16[2,1,16,576]{3,2,1,0:T(8,128)(2,1)}, bf16[2,1,16,576]{3,2,1,0:T(8,128)(2,1)S(1)}, u32[]{:S(2)}, u32[]{:S(2)}) collective-permute-start(bf16[2,1,16,576]{3,2,1,0:T(8,128)(2,1)} %bitcast.11), channel_id=1, source_target_pairs={{0,24},{1,25},{2,26},{3,27},{4,28},{5,29},{6,30},{7,31},{8,16},{9,... | collective-permute-start | bytes 110600 | tf_op jit(solution)/shard_map/ppermute | solution.py:127
  36.0 4.7 %collective-permute-start.7 = (bf16[2,1,16,576]{3,2,1,0:T(8,128)(2,1)}, bf16[2,1,16,576]{3,2,1,0:T(8,128)(2,1)S(1)}, u32[]{:S(2)}, u32[]{:S(2)}) collective-permute-start(bf16[2,1,16,576]{3,2,1,0:T(8,128)(2,1)} %bitcast.12), channel_id=1, source_target_pairs={{0,8},{1,9},{2,10},{3,11},{4,12},{5,13},{6,14},{7,15},{8,0},{9,1},... | collective-permute-start | bytes 110600 | tf_op jit(solution)/shard_map/ppermute | solution.py:127
  36.0 5.1 %collective-permute-start.6 = (bf16[2,1,16,576]{3,2,1,0:T(8,128)(2,1)}, bf16[2,1,16,576]{3,2,1,0:T(8,128)(2,1)S(1)}, u32[]{:S(2)}, u32[]{:S(2)}) collective-permute-start(bf16[2,1,16,576]{3,2,1,0:T(8,128)(2,1)} %bitcast.13), channel_id=1, source_target_pairs={{0,16},{1,17},{2,18},{3,19},{4,20},{5,21},{6,22},{7,23},{8,24},{9,... | collective-permute-start | bytes 110600 | tf_op jit(solution)/shard_map/ppermute | solution.py:127
  36.8 4.3 %copy-start.5 = (bf16[2,16,576]{2,1,0:T(8,128)(2,1)S(1)}, bf16[2,16,576]{2,1,0:T(8,128)(2,1)}, u32[]{:S(2)}) copy-start(bf16[2,16,576]{2,1,0:T(8,128)(2,1)} %get-tuple-element.6) | copy-start | bytes 110596
  37.6 4.0 %collective-permute-start.9 = (f32[16,576]{1,0:T(8,128)S(1)}, f32[16,576]{1,0:T(8,128)S(1)}, u32[]{:S(2)}, u32[]{:S(2)}) collective-permute-start(f32[16,576]{1,0:T(8,128)S(1)} %slice_bitcast_fusion.2), channel_id=1, source_target_pairs={{0,1},{1,0},{2,3},{3,2},{4,5},{5,4},{6,7},{7,6},{8,9},{9,8},{10,11... | collective-permute-start | bytes 110600 | tf_op jit(solution)/shard_map/ppermute | solution.py:127
  41.6 0.6 %copy-start.6 = (f32[16,576]{1,0:T(8,128)}, f32[16,576]{1,0:T(8,128)S(1)}, u32[]{:S(2)}) copy-start(f32[16,576]{1,0:T(8,128)S(1)} %collective-permute-done.9.partner) | copy-start | bytes 110596
  42.2 5.4 %collective-permute-start.12 = (bf16[4,16,576]{2,1,0:T(8,128)(2,1)S(1)}, bf16[4,16,576]{2,1,0:T(8,128)(2,1)S(1)}, u32[]{:S(2)}, u32[]{:S(2)}) collective-permute-start(bf16[4,16,576]{2,1,0:T(8,128)(2,1)S(1)} %get-tuple-element.11), channel_id=1, source_target_pairs={{0,5},{1,4},{2,7},{3,6},{4,1},{5,0},{6,3},{7,2},{8,13},{9,12},{10,... | collective-permute-start | bytes 221192 | tf_op jit(solution)/shard_map/ppermute | solution.py:127
  42.6 5.3 %collective-permute-start.11 = (bf16[4,16,576]{2,1,0:T(8,128)(2,1)S(1)}, bf16[4,16,576]{2,1,0:T(8,128)(2,1)S(1)}, u32[]{:S(2)}, u32[]{:S(2)}) collective-permute-start(bf16[4,16,576]{2,1,0:T(8,128)(2,1)S(1)} %get-tuple-element.10), channel_id=1, source_target_pairs={{0,4},{1,5},{2,6},{3,7},{4,0},{5,1},{6,2},{7,3},{8,12},{9,13},{10,... | collective-permute-start | bytes 221192 | tf_op jit(solution)/shard_map/ppermute | solution.py:127
  44.2 4.4 %collective-permute-start.10 = (bf16[4,16,576]{2,1,0:T(8,128)(2,1)S(1)}, bf16[4,16,576]{2,1,0:T(8,128)(2,1)S(1)}, u32[]{:S(2)}, u32[]{:S(2)}) collective-permute-start(bf16[4,16,576]{2,1,0:T(8,128)(2,1)S(1)} %get-tuple-element.11), channel_id=1, source_target_pairs={{0,1},{1,0},{2,3},{3,2},{4,5},{5,4},{6,7},{7,6},{8,9},{9,8},{10,11... | collective-permute-start | bytes 221192 | tf_op jit(solution)/shard_map/ppermute | solution.py:127
  48.7 1.7 %copy-start.1 = (bf16[16,16,576]{2,1,0:T(8,128)(2,1)}, bf16[16,16,576]{2,1,0:T(8,128)(2,1)S(1)}, u32[]{:S(2)}) copy-start(bf16[16,16,576]{2,1,0:T(8,128)(2,1)S(1)} %pad_maximum_fusion.local) | copy-start | bytes 884740
  48.7 1.7 %collective-permute-start.13 = (bf16[16,16,576]{2,1,0:T(8,128)(2,1)S(1)}, bf16[16,16,576]{2,1,0:T(8,128)(2,1)S(1)}, u32[]{:S(2)}, u32[]{:S(2)}) collective-permute-start(bf16[16,16,576]{2,1,0:T(8,128)(2,1)S(1)} %pad_maximum_fusion.local), channel_id=1, source_target_pairs={{0,2},{1,3},{2,0},{3,1},{4,6},{5,7},{6,4},{7,5},{8,10},{9,11},{10,... | collective-permute-start | bytes 884744 | tf_op jit(solution)/shard_map/ppermute | solution.py:127
  50.4 0.7 %copy-start.4 = (bf16[16,16,576]{2,1,0:T(8,128)(2,1)}, bf16[16,16,576]{2,1,0:T(8,128)(2,1)S(1)}, u32[]{:S(2)}) copy-start(bf16[16,16,576]{2,1,0:T(8,128)(2,1)S(1)} %collective-permute-done.13.other) | copy-start | bytes 884740
